TPU v7x, 32 devices: a whole 2x2x4 slice. The times are simulated.
32 devices in a mesh: stream: 8 (over y, x, core), cross: 4 (over z).
Axes of the slice: x: 2, y: 2, z: 4, core: 2. Of those that a mesh axis runs over, the one named last changes fastest.
Arguments:
- latents: bfloat16 [16384, 128], P(('stream', 'cross')), may hold values from -6 to 6
- stale_latents: bfloat16 [16384, 128], P(('stream', 'cross')), may hold values from -6 to 6
- edge_latents: bfloat16 [49152, 128], P(('stream', 'cross')), may hold values from -6 to 6
- senders: int32 [49152], P(('stream', 'cross')), may hold values from 0 to 1023
- receivers: int32 [49152], P(('stream', 'cross')), may hold values from 0 to 511
- edge_count: int32 [32], P(('stream', 'cross')), may hold values from 512 to 1536, as said below
- send_list: int32 [32, 4, 128], P(('stream', 'cross')), may hold values from 0 to 511
- node_cotangent: bfloat16 [16384, 128], P(('stream', 'cross')), may hold values from -6 to 6
- edge_cotangent: bfloat16 [49152, 128], P(('stream', 'cross')), may hold values from -6 to 6
- edge_first: bfloat16 [384, 128], replicated, may hold values from -0.3125 to 0.3125
- edge_bias: float32 [128], replicated, may hold values from -3 to 3
- edge_second: bfloat16 [128, 128], replicated, may hold values from -0.5 to 0.5
- edge_gain: float32 [128], replicated, may hold values from 0.25 to 1.75
- node_first: bfloat16 [256, 128], replicated, may hold values from -0.375 to 0.375
- node_bias: float32 [128], replicated, may hold values from -3 to 3
- node_second: bfloat16 [128, 128], replicated, may hold values from -0.5 to 0.5
- node_gain: float32 [128], replicated, may hold values from 0.25 to 1.75
Outputs:
- new_latents: bfloat16 [16384, 128], P(('stream', 'cross'))
- latent_grads: bfloat16 [16384, 128], P(('stream', 'cross'))
- stale_grads: bfloat16 [16384, 128], P(('stream', 'cross'))
- edge_grads: bfloat16 [49152, 128], P(('stream', 'cross'))
- edge_first_grad: float32 [384, 128], replicated
- edge_bias_grad: float32 [128], replicated
- edge_second_grad: float32 [128, 128], replicated
- edge_gain_grad: float32 [128], replicated
- node_first_grad: float32 [256, 128], replicated
- node_bias_grad: float32 [128], replicated
- node_second_grad: float32 [128, 128], replicated
- node_gain_grad: float32 [128], replicated
Inputs may be any that keep to these rules, and one draw needn't show every extreme that they name: `edge_count`: a partition's live edge slots come first; some partition has 1536 live slots. `senders`: rows below 512 are the partition's own nodes, the rest its four halo blocks in the order of the steps. `send_list`: a row may be listed more than once.
All inputs are finite; a program needn't handle non-finite values.
Results may differ from a plain program's by a relative error of at most 0.015.
Values may be sent and summed in bfloat16 or wider, within the bound.
No kernel may reach another device: no remote copies, remote signals or barrier semaphores. Data moves between devices by JAX's collectives and lax.ppermute only.
A program may use at most 64 MiB of HBM per device.

v0:
```python
import math

import jax
import jax.numpy as jnp
from jax import lax
from jax.sharding import PartitionSpec as P

EPSILON = 1e-05


def extended(shard, sides, width):
    for axis, dim in sides:
        size, length = (lax.axis_size(axis), shard.shape[dim])
        up = [(i, (i + 1) % size) for i in range(size - 1)]
        down = [(j, i) for i, j in up]
        last = lax.slice_in_dim(shard, length - width, length, axis=dim)
        initial = lax.slice_in_dim(shard, 0, width, axis=dim)
        before = lax.ppermute(last, axis, up)
        after = lax.ppermute(initial, axis, down)
        shard = jnp.concatenate([before, shard, after], axis=dim)
    return shard


def layer_norm(values, scale_gain):
    row_mean = jnp.mean(values, axis=-1, keepdims=True)
    centered = values - row_mean
    variance = jnp.mean(centered * centered, axis=-1, keepdims=True)
    return centered * lax.rsqrt(variance + EPSILON) * scale_gain


def local_layer(owned, halo_rows, edge_rows, params, senders, receivers, edge_total):
    edge_first, edge_bias, edge_second, edge_gain, node_first, node_bias, node_second, node_gain = (
        params
    )
    node_table = jnp.concatenate([owned, halo_rows], axis=0)
    sender_rows = jnp.take(node_table, senders, axis=0)
    receiver_rows = jnp.take(owned, receivers, axis=0)
    joined = jnp.concatenate([edge_rows, sender_rows, receiver_rows], axis=1).astype(jnp.bfloat16)
    hidden_pre = jnp.dot(joined, edge_first, preferred_element_type=jnp.float32) + edge_bias
    edge_hidden = jax.nn.silu(hidden_pre).astype(jnp.bfloat16)
    edge_out = jnp.dot(edge_hidden, edge_second, preferred_element_type=jnp.float32)
    edge_alive = (jnp.arange(edge_rows.shape[0], dtype=jnp.int32) < edge_total).astype(jnp.float32)[
        :, None
    ]
    new_edges = (edge_rows + edge_alive * layer_norm(edge_out, edge_gain)).astype(jnp.bfloat16)
    summed = (
        jnp.zeros(owned.shape, jnp.float32)
        .at[receivers]
        .add(edge_alive * new_edges.astype(jnp.float32))
    )
    node_input = jnp.concatenate([owned, summed], axis=1).astype(jnp.bfloat16)
    node_pre = jnp.dot(node_input, node_first, preferred_element_type=jnp.float32) + node_bias
    node_hidden = jax.nn.silu(node_pre).astype(jnp.bfloat16)
    node_out = jnp.dot(node_hidden, node_second, preferred_element_type=jnp.float32)
    new_latents = (owned + layer_norm(node_out, node_gain)).astype(jnp.bfloat16)
    return (new_latents, new_edges)


def local_step(
    latent_block, halo_block, edge_block, params, senders, receivers, edge_total, node_cot, edge_cot
):

    def forward(owned, halo_rows, edge_rows, weights):
        return local_layer(owned, halo_rows, edge_rows, weights, senders, receivers, edge_total)

    outputs, pullback = jax.vjp(
        forward,
        latent_block.astype(jnp.float32),
        halo_block.astype(jnp.float32),
        edge_block.astype(jnp.float32),
        params,
    )
    grad_owned, grad_halo, grad_edges, grad_params = pullback((node_cot, edge_cot))
    grad_params = tuple((item.astype(jnp.float32) for item in grad_params))
    return (outputs[0], grad_owned, grad_halo, grad_edges, grad_params)


def per_device(
    latents,
    stale_latents,
    edge_latents,
    senders,
    receivers,
    edge_count,
    send_list,
    node_cotangent,
    edge_cotangent,
    edge_first,
    edge_bias,
    edge_second,
    edge_gain,
    node_first,
    node_bias,
    node_second,
    node_gain,
):
    depth = send_list.shape[2]
    width = latents.shape[1]
    send_rows = send_list[0].reshape(-1)
    picked = jnp.take(stale_latents, send_rows, axis=0).reshape(4, depth, width)
    stream_pair = jnp.concatenate([picked[1], picked[0]], axis=0)
    cross_pair = jnp.concatenate([picked[3], picked[2]], axis=0)
    along = extended(stream_pair, (("stream", 0),), depth)
    across = extended(cross_pair, (("cross", 0),), depth)
    halo_rows = jnp.concatenate(
        [along[:depth], along[3 * depth :], across[:depth], across[3 * depth :]], axis=0
    )
    params = (
        edge_first,
        edge_bias,
        edge_second,
        edge_gain,
        node_first,
        node_bias,
        node_second,
        node_gain,
    )
    new_latents, grad_owned, grad_halo, grad_edges, grad_params = local_step(
        latents,
        halo_rows,
        edge_latents,
        params,
        senders,
        receivers,
        edge_count[0],
        node_cotangent,
        edge_cotangent,
    )
    halo_grads = grad_halo.reshape(4, depth, width)
    back_stream = extended(
        jnp.concatenate([halo_grads[0], halo_grads[1]], axis=0).astype(jnp.bfloat16),
        (("stream", 0),),
        depth,
    ).astype(jnp.float32)
    back_cross = extended(
        jnp.concatenate([halo_grads[2], halo_grads[3]], axis=0).astype(jnp.bfloat16),
        (("cross", 0),),
        depth,
    ).astype(jnp.float32)
    returned = jnp.concatenate(
        [
            back_stream[3 * depth :],
            back_stream[:depth],
            back_cross[3 * depth :],
            back_cross[:depth],
        ],
        axis=0,
    )
    stale_grads = (
        jnp.zeros(latents.shape, jnp.float32).at[send_rows].add(returned).astype(jnp.bfloat16)
    )
    entries = 0
    for item in grad_params:
        entries = entries + item.size
    limit = math.sqrt(entries)
    totals = lax.psum(grad_params, ("stream", "cross"))
    squares = jnp.zeros((), jnp.float32)
    for item in totals:
        squares = squares + jnp.sum(item * item)
    factor = jnp.minimum(1.0, limit * lax.rsqrt(squares))
    clipped = tuple((item * factor for item in totals))
    return (
        new_latents,
        grad_owned.astype(jnp.bfloat16),
        stale_grads,
        grad_edges.astype(jnp.bfloat16),
        clipped[0],
        clipped[1],
        clipped[2],
        clipped[3],
        clipped[4],
        clipped[5],
        clipped[6],
        clipped[7],
    )


def solution(mesh):
    in_specs = (
        P(("stream", "cross"), None),
        P(("stream", "cross"), None),
        P(("stream", "cross"), None),
        P(("stream", "cross")),
        P(("stream", "cross")),
        P(("stream", "cross")),
        P(("stream", "cross"), None, None),
        P(("stream", "cross"), None),
        P(("stream", "cross"), None),
        P(),
        P(),
        P(),
        P(),
        P(),
        P(),
        P(),
        P(),
    )
    out_specs = (
        P(("stream", "cross"), None),
        P(("stream", "cross"), None),
        P(("stream", "cross"), None),
        P(("stream", "cross"), None),
        P(),
        P(),
        P(),
        P(),
        P(),
        P(),
        P(),
        P(),
    )
    return jax.shard_map(
        per_device, mesh=mesh, in_specs=in_specs, out_specs=out_specs, check_vma=False
    )
```

profile of v0, /device:TPU:1, one launch (start us, length us, event | category | flops | bytes accessed | tf_op | source)
XLA Modules:
  0.0 292.3 jit_solution(8887668701360947818)
XLA Ops:
  7.2 0.7 compare_and_fusion.2
  8.0 0.7 compare_select_fusion.2
  9.3 1.3 gather_fusion
  10.8 4.5 %collective-permute-start = (bf16[128,128]{0,1:T(8,128)(2,1)S(1)}, bf16[128,128]{0,1:T(8,128)(2,1)S(1)}, u32[]{:S(2)}, u32[]{:S(2)}) collective-permute-start(bf16[128,128]{0,1:T(8,128)(2,1)S(1)} %get-tuple-element.66), channel_id=1, source_target_pairs={{0,4},{4,8},{8,12},{12,16},{16,20},{20,24},{24,28},{1,5},{5,9},{9,... | collective-permute-start | bytes 98312 | tf_op jit(solution)/shard_map/ppermute | solution.py:18
  15.3 1.3 collective-permute-start.3
  16.6 4.0 %collective-permute-start.2 = (bf16[128,128]{0,1:T(8,128)(2,1)S(1)}, bf16[128,128]{0,1:T(8,128)(2,1)S(1)}, u32[]{:S(2)}, u32[]{:S(2)}) collective-permute-start(bf16[128,128]{0,1:T(8,128)(2,1)S(1)} %get-tuple-element.68), channel_id=1, source_target_pairs={{0,1},{1,2},{2,3},{4,5},{5,6},{6,7},{8,9},{9,10},{10,11},{12,13},{... | collective-permute-start | bytes 98312 | tf_op jit(solution)/shard_map/ppermute | solution.py:18
  20.6 1.9 collective-permute-start.1
  22.5 0.7 compare_and_fusion
  23.2 0.7 compare_select_fusion.1
  23.9 0.7 compare_and_fusion.1
  24.6 0.7 compare_select_fusion
  26.1 1.0 copy.55
  27.3 3.2 %gather_fusion.2 = bf16[1536,128]{1,0:T(8,128)(2,1)S(1)} fusion(bf16[512,128]{1,0:T(8,128)(2,1)S(1)} %copy.51, s32[2048]{0:T(1024)S(1)} %pad_clamp_fusion), kind=kCustom, calls=%fused_computation.2 | custom fusion | bytes 792576 | tf_op jit(solution)/shard_map/jvp(jit(_take))/gather | solution.py:37
  31.5 3.2 %gather_fusion.1 = bf16[1536,128]{1,0:T(8,128)(2,1)S(1)} fusion(bf16[1024,128]{1,0:T(8,128)(2,1)S(1)} %copy.49, s32[2048]{0:T(1024)S(1)} %pad_clamp_fusion.1), kind=kCustom, calls=%fused_computation.1 | custom fusion | bytes 792576 | tf_op jit(solution)/shard_map/jvp(jit(_take))/gather | solution.py:36
  35.1 1.4 multiply_convert_fusion.1
  37.8 9.1 %scatter_custom_fusion = f32[512,128]{1,0:T(8,128)S(1)} fusion(s32[1536]{0:T(1024)} %copy-done.24, f32[1536,128]{1,0:T(8,128)S(1)} %copy.54, f32[]{:T(128)} %constant.42.clone.1), kind=kCustom, calls=%fused_computation.89 | custom fusion | flops 196608 | bytes 262656 | tf_op jit(solution)/shard_map/jvp()/scatter-add | solution.py:49
  47.7 1.3 fusion.26
  49.0 0.9 fusion.7
  49.9 0.9 fusion.65
  50.8 0.9 fusion.5
  51.9 0.8 copy-done.1
  52.9 2.6 gather_fusion.3
  56.2 0.9 fusion.13
  57.1 1.1 fusion.6
  58.3 1.1 fusion.64
  59.5 1.1 fusion.4
  61.6 9.0 %scatter_custom_fusion.1 = f32[1024,128]{1,0:T(8,128)S(1)} fusion(s32[1536]{0:T(1024)} %copy-done.28, f32[1536,128]{1,0:T(8,128)S(1)} %copy.61, f32[]{:T(128)} %constant.42.clone.1), kind=kCustom, calls=%fused_computation.75 | custom fusion | flops 196608 | bytes 524800 | tf_op jit(solution)/shard_map/transpose(jvp(jit(_take)))/scatter-add | solution.py:36
  70.8 39.6 %all-reduce = (f32[128]{0:T(128)S(1)}, f32[128]{0:T(128)S(1)}, f32[128]{0:T(128)S(1)}, f32[128]{0:T(128)S(1)}) all-reduce(f32[128]{0:T(128)S(1)} %copy-done.38, f32[128]{0:T(128)S(1)} %copy-done.34, f32[128]{0:T(128)S(1)} %copy-done.37, f32[128]{0:T(128)S(1)} %copy-done.36), channel_id=1, replica_groups=mesh['stream'=8,'cross'=4] {'stream','cross'}, use_global_device_ids=true, to_apply=%region_15.16 | all-reduce | flops 512 | bytes 4096 | tf_op jit(solution)/shard_map/psum | solution.py:156
  111.1 0.7 multiply_reduce_fusion.7
  112.5 1.3 collective-permute-start.7
  113.8 4.0 %collective-permute-start.6 = (bf16[128,128]{1,0:T(8,128)(2,1)S(1)}, bf16[128,128]{1,0:T(8,128)(2,1)S(1)}, u32[]{:S(2)}, u32[]{:S(2)}) collective-permute-start(bf16[128,128]{1,0:T(8,128)(2,1)S(1)} %get-tuple-element.58), channel_id=1, source_target_pairs={{0,1},{1,2},{2,3},{4,5},{5,6},{6,7},{8,9},{9,10},{10,11},{12,13},{... | collective-permute-start | bytes 98312 | tf_op jit(solution)/shard_map/ppermute | solution.py:18
  118.4 0.8 copy.65
  119.2 0.9 copy.66
  120.5 8.9 %scatter_fusion = f32[512,128]{1,0:T(8,128)S(1)} fusion(f32[512,128]{1,0:T(8,128)S(1)} %copy.63, s32[1536]{0:T(1024)S(1)} %copy-done.25, f32[1536,128]{1,0:T(8,128)S(1)} %copy.64), kind=kCustom, calls=%fused_computation.6 | custom fusion | flops 196608 | bytes 2365440 | tf_op jit(solution)/shard_map/transpose(jvp(jit(_take)))/scatter-add | solution.py:37
  129.4 0.7 convert_element_type.127
  130.1 5.8 %collective-permute-start.4 = (bf16[128,128]{1,0:T(8,128)(2,1)S(1)}, bf16[128,128]{1,0:T(8,128)(2,1)S(1)}, u32[]{:S(2)}, u32[]{:S(2)}) collective-permute-start(bf16[128,128]{1,0:T(8,128)(2,1)S(1)} %get-tuple-element.56), channel_id=1, source_target_pairs={{0,4},{4,8},{8,12},{12,16},{16,20},{20,24},{24,28},{1,5},{5,9},{9,... | collective-permute-start | bytes 98312 | tf_op jit(solution)/shard_map/ppermute | solution.py:18
  135.9 1.9 collective-permute-start.5
  137.9 3.2 %collective-permute-done.5 = bf16[128,128]{1,0:T(8,128)(2,1)S(1)} collective-permute-done((bf16[128,128]{1,0:T(8,128)(2,1)S(1)}, bf16[128,128]{1,0:T(8,128)(2,1)S(1)}, u32[]{:S(2)}, u32[]{:S(2)}) %collective-permute-start.5) | collective-permute-done | bytes 32800 | tf_op jit(solution)/shard_map/ppermute | solution.py:19
  141.2 2.5 scatter_custom_fusion.3
  144.3 121.6 %all-reduce.4.cloned.1.call-done = (f32[384,128]{1,0:T(8,128)}, f32[128,128]{1,0:T(8,128)}, f32[256,128]{1,0:T(8,128)}, f32[128,128]{1,0:T(8,128)}) async-done(((f32[384,128]{1,0:T(8,128)}, f32[128,128]{1,0:T(8,128)}, f32[256,128]{1,0:T(8,128)}, f32[128,128]{1,0:T(8,128)}), (f32[384,128]{1,0:T(8,128)}, f32[128,128]{1,0:T(8,128)}, f32[256,128]{1,0:T(8,128)}, ...) | async-done | bytes 458768 | tf_op jit(solution)/shard_map/psum | solution.py:156
  265.9 1.5 multiply_reduce_fusion.4
  267.4 1.5 multiply_reduce_fusion.3
  268.9 1.5 multiply_reduce_fusion.5
  270.4 1.6 multiply_reduce_fusion.2
  278.8 1.5 broadcast_multiply_fusion.2
  280.3 1.6 broadcast_multiply_fusion.1
  281.9 1.5 broadcast_multiply_fusion.3
  283.8 1.6 broadcast_multiply_fusion
  (152 shorter events, 11.4 us)
Async XLA Ops:
  7.2 2.1 copy-start
  7.2 19.9 %copy-start.5 = (bf16[512,128]{1,0:T(8,128)(2,1)S(1)}, bf16[512,128]{1,0:T(8,128)(2,1)}, u32[]{:S(2)}) copy-start(bf16[512,128]{1,0:T(8,128)(2,1)} %param.17) | copy-start | bytes 393220
  7.2 258.7 %all-reduce.4.cloned.1.call-start = ((), (), s32[]{:S(2)}) async-start(), calls=%async_computation | async-start | bytes 917504 | tf_op jit(solution)/shard_map/psum | solution.py:156
  10.8 20.4 %collective-permute-start = (bf16[128,128]{0,1:T(8,128)(2,1)S(1)}, bf16[128,128]{0,1:T(8,128)(2,1)S(1)}, u32[]{:S(2)}, u32[]{:S(2)}) collective-permute-start(bf16[128,128]{0,1:T(8,128)(2,1)S(1)} %get-tuple-element.66), channel_id=1, source_target_pairs={{0,4},{4,8},{8,12},{12,16},{16,20},{20,24},{24,28},{1,5},{5,9},{9,... | collective-permute-start | bytes 98312 | tf_op jit(solution)/shard_map/ppermute | solution.py:18
  15.3 15.9 %collective-permute-start.3 = (bf16[128,128]{0,1:T(8,128)(2,1)S(1)}, bf16[128,128]{0,1:T(8,128)(2,1)S(1)}, u32[]{:S(2)}, u32[]{:S(2)}) collective-permute-start(bf16[128,128]{0,1:T(8,128)(2,1)S(1)} %get-tuple-element.67), channel_id=1, source_target_pairs={{1,0},{2,1},{3,2},{5,4},{6,5},{7,6},{9,8},{10,9},{11,10},{13,12},{... | collective-permute-start | bytes 98312 | tf_op jit(solution)/shard_map/ppermute | solution.py:19
  16.6 14.6 %collective-permute-start.2 = (bf16[128,128]{0,1:T(8,128)(2,1)S(1)}, bf16[128,128]{0,1:T(8,128)(2,1)S(1)}, u32[]{:S(2)}, u32[]{:S(2)}) collective-permute-start(bf16[128,128]{0,1:T(8,128)(2,1)S(1)} %get-tuple-element.68), channel_id=1, source_target_pairs={{0,1},{1,2},{2,3},{4,5},{5,6},{6,7},{8,9},{9,10},{10,11},{12,13},{... | collective-permute-start | bytes 98312 | tf_op jit(solution)/shard_map/ppermute | solution.py:18
  20.6 10.6 %collective-permute-start.1 = (bf16[128,128]{0,1:T(8,128)(2,1)S(1)}, bf16[128,128]{0,1:T(8,128)(2,1)S(1)}, u32[]{:S(2)}, u32[]{:S(2)}) collective-permute-start(bf16[128,128]{0,1:T(8,128)(2,1)S(1)} %get-tuple-element.69), channel_id=1, source_target_pairs={{4,0},{8,4},{12,8},{16,12},{20,16},{24,20},{28,24},{5,1},{9,5},{13... | collective-permute-start | bytes 98312 | tf_op jit(solution)/shard_map/ppermute | solution.py:19
  23.2 11.6 %copy-start.29 = (pred[1536]{0:T(1024)(128)(4,1)}, pred[1536]{0:T(1024)(128)(4,1)S(1)}, u32[]{:S(2)}) copy-start(pred[1536]{0:T(1024)(128)(4,1)S(1)} %compare_and_fusion) | copy-start | bytes 4612
  23.9 2.1 copy-start.24
  25.3 5.4 %copy-start.28 = (s32[1536]{0:T(1024)}, s32[1536]{0:T(1024)S(1)}, u32[]{:S(2)}) copy-start(s32[1536]{0:T(1024)S(1)} %compare_select_fusion) | copy-start | bytes 18436
  26.0 4.7 %copy-start.22 = (s32[2048]{0:T(1024)}, s32[2048]{0:T(1024)S(1)}, u32[]{:S(2)}) copy-start(s32[2048]{0:T(1024)S(1)} %pad_clamp_fusion) | copy-start | bytes 24580
  27.2 3.6 %copy-start.7 = (bf16[1536,128]{1,0:T(8,128)(2,1)S(1)}, bf16[1536,128]{1,0:T(8,128)(2,1)}, u32[]{:S(2)}) copy-start(bf16[1536,128]{1,0:T(8,128)(2,1)} %param.19) | copy-start | bytes 1179652
  27.3 3.6 %copy-start.8 = (bf16[1536,128]{1,0:T(8,128)(2,1)S(1)}, bf16[1536,128]{1,0:T(8,128)(2,1)}, u32[]{:S(2)}) copy-start(bf16[1536,128]{1,0:T(8,128)(2,1)} %param.25) | copy-start | bytes 1179652
  31.0 6.3 %copy-start.3 = (bf16[1536,128]{0,1:T(8,128)(2,1)}, bf16[1536,128]{0,1:T(8,128)(2,1)S(1)}, u32[]{:S(2)}) copy-start(bf16[1536,128]{0,1:T(8,128)(2,1)S(1)} %copy.47) | copy-start | bytes 1179652
  31.4 3.6 %copy-start.16 = (bf16[384,128]{1,0:T(8,128)(2,1)S(1)}, bf16[384,128]{1,0:T(8,128)(2,1)}, u32[]{:S(2)}) copy-start(bf16[384,128]{1,0:T(8,128)(2,1)} %param.26) | copy-start | bytes 294916
  31.5 3.6 %copy-start.41 = (f32[128]{0:T(128)S(1)}, f32[128]{0:T(128)}, u32[]{:S(2)}) copy-start(f32[128]{0:T(128)} %param.27) | copy-start | bytes 1540
  35.0 1.5 copy-start.9
  35.0 1.5 copy-start.11
  35.1 1.5 copy-start.26
  35.1 2.2 copy-start.32
  36.9 10.1 %copy-start.15 = (bf16[256,128]{1,0:T(8,128)(2,1)S(1)}, bf16[256,128]{1,0:T(8,128)(2,1)}, u32[]{:S(2)}) copy-start(bf16[256,128]{1,0:T(8,128)(2,1)} %param.30) | copy-start | bytes 196612
  36.9 10.1 %copy-start.39 = (f32[128]{0:T(128)S(1)}, f32[128]{0:T(128)}, u32[]{:S(2)}) copy-start(f32[128]{0:T(128)} %param.31) | copy-start | bytes 1540
  37.3 9.9 %copy-start.20 = (f32[1536]{0:T(1024)}, f32[1536]{0:T(1024)S(1)}, u32[]{:S(2)}) copy-start(f32[1536]{0:T(1024)S(1)} %multiply_reduce_fusion) | copy-start | bytes 18436
  37.3 9.9 %copy-start.18 = (f32[1536]{0:T(1024)}, f32[1536]{0:T(1024)S(1)}, u32[]{:S(2)}) copy-start(f32[1536]{0:T(1024)S(1)} %fusion.49) | copy-start | bytes 18436
  37.3 9.9 %copy-start.40 = (bf16[128,128]{1,0:T(8,128)(2,1)S(1)}, bf16[128,128]{1,0:T(8,128)(2,1)}, u32[]{:S(2)}) copy-start(bf16[128,128]{1,0:T(8,128)(2,1)} %param.32) | copy-start | bytes 98308
  37.5 10.0 %copy-start.35 = (f32[128]{0:T(128)S(1)}, f32[128]{0:T(128)}, u32[]{:S(2)}) copy-start(f32[128]{0:T(128)} %param.33) | copy-start | bytes 1540
  49.9 3.0 %copy-start.23 = (s32[2048]{0:T(1024)S(1)}, s32[2048]{0:T(1024)}, u32[]{:S(2)}) copy-start(s32[2048]{0:T(1024)} %copy-done.22) | copy-start | bytes 24580
  51.9 0.8 copy-start.1
  52.9 2.9 %copy-start.30 = (pred[1536]{0:T(1024)(128)(4,1)S(1)}, pred[1536]{0:T(1024)(128)(4,1)}, u32[]{:S(2)}) copy-start(pred[1536]{0:T(1024)(128)(4,1)} %copy-done.29) | copy-start | bytes 4612
  52.9 2.9 %copy-start.33 = (f32[128]{0:T(128)S(1)}, f32[128]{0:T(128)}, u32[]{:S(2)}) copy-start(f32[128]{0:T(128)} %param.29) | copy-start | bytes 1540
  55.8 1.3 copy-start.14
  55.8 2.4 copy-start.27
  55.9 2.4 copy-start.42
  58.2 1.2 copy-start.4
  58.2 1.2 copy-start.10
  58.3 1.2 copy-start.12
  59.4 1.2 copy-start.17
  61.3 9.5 %copy-start.34 = (f32[128]{0:T(128)S(1)}, f32[128]{0:T(128)}, u32[]{:S(2)}) copy-start(f32[128]{0:T(128)} %get-tuple-element.36) | copy-start | bytes 1540
  61.3 9.5 %copy-start.36 = (f32[128]{0:T(128)S(1)}, f32[128]{0:T(128)}, u32[]{:S(2)}) copy-start(f32[128]{0:T(128)} %get-tuple-element.38) | copy-start | bytes 1540
  61.3 9.4 %copy-start.37 = (f32[128]{0:T(128)S(1)}, f32[128]{0:T(128)}, u32[]{:S(2)}) copy-start(f32[128]{0:T(128)} %get-tuple-element.80) | copy-start | bytes 1540
  61.4 9.4 %copy-start.38 = (f32[128]{0:T(128)S(1)}, f32[128]{0:T(128)}, u32[]{:S(2)}) copy-start(f32[128]{0:T(128)} %get-tuple-element.78) | copy-start | bytes 1540
  61.4 51.1 %copy-start.2 = (f32[512,256]{0,1:T(8,128)S(1)}, f32[512,256]{0,1:T(8,128)}, u32[]{:S(2)}) copy-start(f32[512,256]{0,1:T(8,128)} %copy-done.1) | copy-start | bytes 1572868
  70.6 47.8 %copy-start.6 = (bf16[512,128]{0,1:T(8,128)(2,1)S(1)}, bf16[512,128]{0,1:T(8,128)(2,1)}, u32[]{:S(2)}) copy-start(bf16[512,128]{0,1:T(8,128)(2,1)} %get-tuple-element.55) | copy-start | bytes 393220
  70.8 49.8 %copy-start.25 = (s32[1536]{0:T(1024)S(1)}, s32[1536]{0:T(1024)}, u32[]{:S(2)}) copy-start(s32[1536]{0:T(1024)} %copy-done.24) | copy-start | bytes 18436
  112.5 25.3 %collective-permute-start.7 = (bf16[128,128]{1,0:T(8,128)(2,1)S(1)}, bf16[128,128]{1,0:T(8,128)(2,1)S(1)}, u32[]{:S(2)}, u32[]{:S(2)}) collective-permute-start(bf16[128,128]{1,0:T(8,128)(2,1)S(1)} %get-tuple-element.57), channel_id=1, source_target_pairs={{1,0},{2,1},{3,2},{5,4},{6,5},{7,6},{9,8},{10,9},{11,10},{13,12},{... | collective-permute-start | bytes 98312 | tf_op jit(solution)/shard_map/ppermute | solution.py:19
  113.8 24.0 %collective-permute-start.6 = (bf16[128,128]{1,0:T(8,128)(2,1)S(1)}, bf16[128,128]{1,0:T(8,128)(2,1)S(1)}, u32[]{:S(2)}, u32[]{:S(2)}) collective-permute-start(bf16[128,128]{1,0:T(8,128)(2,1)S(1)} %get-tuple-element.58), channel_id=1, source_target_pairs={{0,1},{1,2},{2,3},{4,5},{5,6},{6,7},{8,9},{9,10},{10,11},{12,13},{... | collective-permute-start | bytes 98312 | tf_op jit(solution)/shard_map/ppermute | solution.py:18
  130.1 7.8 %collective-permute-start.4 = (bf16[128,128]{1,0:T(8,128)(2,1)S(1)}, bf16[128,128]{1,0:T(8,128)(2,1)S(1)}, u32[]{:S(2)}, u32[]{:S(2)}) collective-permute-start(bf16[128,128]{1,0:T(8,128)(2,1)S(1)} %get-tuple-element.56), channel_id=1, source_target_pairs={{0,4},{4,8},{8,12},{12,16},{16,20},{20,24},{24,28},{1,5},{5,9},{9,... | collective-permute-start | bytes 98312 | tf_op jit(solution)/shard_map/ppermute | solution.py:18
  135.9 5.2 %collective-permute-start.5 = (bf16[128,128]{1,0:T(8,128)(2,1)S(1)}, bf16[128,128]{1,0:T(8,128)(2,1)S(1)}, u32[]{:S(2)}, u32[]{:S(2)}) collective-permute-start(bf16[128,128]{1,0:T(8,128)(2,1)S(1)} %get-tuple-element.59), channel_id=1, source_target_pairs={{4,0},{8,4},{12,8},{16,12},{20,16},{24,20},{28,24},{5,1},{9,5},{13... | collective-permute-start | bytes 98312 | tf_op jit(solution)/shard_map/ppermute | solution.py:19
  (4 other events, 2.7 us)
Sparse Core Ops, SparseCore 0:
  138.0 127.9 all-reduce.3
where the time goes:
time: 293 us; the launch traced here: 292 us
  waiting for transfers between devices  125 us (43%)
  other arithmetic  55.3 us (19%)
  blocking collectives  39.6 us (14%)
  starting transfers between devices  24.8 us (8%)
  between operations  21 us (7%)
  local copies, waits for them, and re-layouts  17.7 us (6%)
  matrix products  9 us (3%)
    psum x1, waiting for transfers between devices, per_device(): totals = lax.psum(grad_params, ('stream', 'cross'))  122 us
    psum x1, blocking collectives, per_device(): totals = lax.psum(grad_params, ('stream', 'cross'))  39.6 us
    ppermute x4, starting transfers between devices, extended(): before = lax.ppermute(last, axis, up)  18.3 us
    scatter-add x1, other arithmetic, local_layer(): summed = jnp.zeros(owned.shape, jnp.float32).at[receivers].add(edge_alive...  9.11 us
    scatter-add x1, other arithmetic, local_layer(): sender_rows = jnp.take(node_table, senders, axis=0)  9 us
    scatter-add x1, other arithmetic, local_layer(): receiver_rows = jnp.take(owned, receivers, axis=0)  8.87 us
    reduce_sum x8, other arithmetic, per_device(): squares = squares + jnp.sum(item * item)  8.58 us
    mul x8, other arithmetic, per_device(): clipped = tuple((item * factor for item in totals))  8.18 us
  transfers between devices with their start and end apart: 9, of which 2 were waited for; matrix products, arithmetic and copies ran while one was open for 8% of the time, Pallas kernels for 0%

commit v1 on v0

v1 whole, which is shorter than its diff:
```python
import functools
import math

import jax
import jax.numpy as jnp
from jax import lax
from jax.experimental import pallas as pl
from jax.experimental.pallas import tpu as pltpu
from jax.sharding import PartitionSpec as P

EPSILON = 1e-05
BF = jnp.bfloat16
F32 = jnp.float32
VMEM_LIMIT = 40 * 1024 * 1024


def mm(a, b):
    return jnp.dot(a, b, preferred_element_type=F32)


def mm_nt(a, b):
    return lax.dot_general(a, b, (((1,), (1,)), ((), ())), preferred_element_type=F32)


def mm_tn(a, b):
    return lax.dot_general(a, b, (((0,), (0,)), ((), ())), preferred_element_type=F32)


def index_columns(index_ref, row):
    line = index_ref[row : row + 1, :].astype(F32)
    return jnp.broadcast_to(line, (line.shape[1], line.shape[1])).T


def one_hot_rows(column, size):
    lanes = column.shape[1]
    lane = lax.broadcasted_iota(jnp.int32, column.shape, 1).astype(F32)
    blocks = [
        jnp.where(column == lane + float(base), 1.0, 0.0).astype(BF)
        for base in range(0, size, lanes)
    ]
    return jnp.concatenate(blocks, axis=1)


def one_hot_columns(index_ref, row, size):
    line = index_ref[row : row + 1, :]
    place = lax.broadcasted_iota(jnp.int32, (size, line.shape[1]), 0)
    return jnp.where(place == line, 1.0, 0.0).astype(BF)


def pick_kernel(list_ref, stale_ref, out_ref):
    width = list_ref.shape[1]
    for block in range(list_ref.shape[0]):
        hot = one_hot_rows(index_columns(list_ref, block), stale_ref.shape[0])
        out_ref[block] = mm(hot, stale_ref[...]).astype(BF)


def stale_kernel(list_ref, b0, b1, b2, b3, out_ref):
    total = None
    for block, part in enumerate((b0, b1, b2, b3)):
        hot = one_hot_columns(list_ref, block, out_ref.shape[0])
        piece = mm(hot, part[...])
        total = piece if total is None else total + piece
    out_ref[...] = total.astype(BF)


def norm_forward(z):
    mean = jnp.mean(z, axis=-1, keepdims=True)
    centered = z - mean
    variance = jnp.mean(centered * centered, axis=-1, keepdims=True)
    inverse = lax.rsqrt(variance + EPSILON)
    return centered * inverse, jnp.broadcast_to(inverse, z.shape)


def norm_backward(slope, unit, inverse):
    first = jnp.mean(slope, axis=-1, keepdims=True)
    second = jnp.mean(slope * unit, axis=-1, keepdims=True)
    return inverse * (slope - first - unit * second)


def silu_pair(v):
    sig = 1.0 / (1.0 + jnp.exp(-v))
    hidden = v * sig
    return hidden, sig + hidden * (1.0 - sig)


def main_kernel(
    count_ref,
    latents,
    h0,
    h1,
    h2,
    h3,
    edges,
    senders,
    receivers,
    node_cot,
    edge_cot,
    edge_first,
    edge_bias,
    edge_second,
    edge_gain,
    node_first,
    node_bias,
    node_second,
    node_gain,
    new_latents,
    latent_grads,
    edge_grads,
    halo_grads,
    packed,
    table,
    hot_recv,
    turn_recv,
    turn_send,
    send_rows,
    recv_rows,
    hidden_s,
    slope_s,
    unit_s,
    inverse_s,
    alive_edges,
    dz_s,
    dpre_s,
):
    n, w = latents.shape
    e = edges.shape[0]
    t = table.shape[0]
    depth = h0.shape[0]
    total = count_ref[0]
    chunk = 2 * w
    table[:n] = latents[...]
    for i, part in enumerate((h0, h1, h2, h3)):
        table[n + i * depth : n + (i + 1) * depth] = part[...]
    gain = edge_gain[...]

    for c in range(e // chunk):
        rows = slice(c * chunk, (c + 1) * chunk)
        for b in range(chunk // w):
            row = c * (chunk // w) + b
            part = slice(row * w, (row + 1) * w)
            hot = one_hot_rows(index_columns(senders, row), t)
            send_rows[part] = mm(hot, table[...]).astype(BF)
            hot = one_hot_rows(index_columns(receivers, row), n)
            hot_recv[part] = hot
            recv_rows[part] = mm(hot, latents[...]).astype(BF)
            turn_send[:, part] = one_hot_columns(senders, row, t)
            turn_recv[:, part] = one_hot_columns(receivers, row, n)
        edge = edges[rows]
        pre = (
            mm(edge, edge_first[:w])
            + mm(send_rows[rows], edge_first[w : 2 * w])
            + mm(recv_rows[rows], edge_first[2 * w :])
            + edge_bias[...]
        )
        hidden, slope = silu_pair(pre)
        hidden = hidden.astype(BF)
        hidden_s[rows] = hidden
        slope_s[rows] = slope
        unit, inverse = norm_forward(mm(hidden, edge_second[...]))
        unit_s[rows] = unit
        inverse_s[rows] = inverse
        place = lax.broadcasted_iota(jnp.int32, (chunk, w), 0) + c * chunk
        fresh = (edge.astype(F32) + unit * gain).astype(BF)
        alive_edges[rows] = jnp.where(place < total, fresh, jnp.zeros_like(fresh))

    aggregate = mm(turn_recv[...], alive_edges[...]).astype(BF)
    own = latents[...]
    hidden, slope = silu_pair(mm(own, node_first[:w]) + mm(aggregate, node_first[w:]) + node_bias[...])
    hidden = hidden.astype(BF)
    unit, inverse = norm_forward(mm(hidden, node_second[...]))
    new_latents[...] = (own.astype(F32) + unit * node_gain[...]).astype(BF)
    ncot = node_cot[...].astype(F32)
    node_gain_grad = jnp.sum(ncot * unit, axis=0, keepdims=True)
    dz = norm_backward(ncot * node_gain[...], unit, inverse).astype(BF)
    dpre = mm_nt(dz, node_second[...]) * slope
    node_bias_grad = jnp.sum(dpre, axis=0, keepdims=True)
    dpre = dpre.astype(BF)
    d_aggregate = mm_nt(dpre, node_first[w:]).astype(BF)
    latent_part = ncot + mm_nt(dpre, node_first[:w])
    at = 4 * w
    packed[at : at + w] = mm_tn(own, dpre).astype(BF)
    packed[at + w : at + 2 * w] = mm_tn(aggregate, dpre).astype(BF)
    packed[at + 2 * w : at + 3 * w] = mm_tn(hidden, dz).astype(BF)

    bias_grad = jnp.zeros((1, w), F32)
    gain_grad = jnp.zeros((1, w), F32)
    for c in range(e // chunk):
        rows = slice(c * chunk, (c + 1) * chunk)
        place = lax.broadcasted_iota(jnp.int32, (chunk, w), 0) + c * chunk
        alive = place < total
        passed = mm(hot_recv[rows], d_aggregate)
        cot = edge_cot[rows].astype(F32) + jnp.where(alive, passed, 0.0)
        live = jnp.where(alive, cot, 0.0)
        unit = unit_s[rows]
        gain_grad = gain_grad + jnp.sum(live * unit, axis=0, keepdims=True)
        dz = norm_backward(live * gain, unit, inverse_s[rows]).astype(BF)
        dz_s[rows] = dz
        dpre = mm_nt(dz, edge_second[...]) * slope_s[rows]
        bias_grad = bias_grad + jnp.sum(dpre, axis=0, keepdims=True)
        dpre = dpre.astype(BF)
        dpre_s[rows] = dpre
        edge_grads[rows] = (cot + mm_nt(dpre, edge_first[:w])).astype(BF)

    dpre = dpre_s[...]
    packed[:w] = mm_tn(edges[...], dpre).astype(BF)
    packed[w : 2 * w] = mm_tn(send_rows[...], dpre).astype(BF)
    packed[2 * w : 3 * w] = mm_tn(recv_rows[...], dpre).astype(BF)
    packed[3 * w : 4 * w] = mm_tn(hidden_s[...], dz_s[...]).astype(BF)
    tail = jnp.concatenate(
        [bias_grad, gain_grad, node_bias_grad, node_gain_grad, jnp.zeros((w - 4, w), F32)], axis=0
    )
    packed[7 * w :] = tail.astype(BF)

    from_send = mm(turn_send[...], dpre).astype(BF)
    from_recv = mm(turn_recv[...], dpre).astype(BF)
    back = mm_nt(from_send, edge_first[w : 2 * w])
    latent_grads[...] = (
        latent_part + back[:n] + mm_nt(from_recv, edge_first[2 * w :])
    ).astype(BF)
    halo_grads[...] = back[n:].astype(BF)


def final_kernel(limit, bit_ref, mine, other, *outs):
    swap = bit_ref[0] == 1
    a, b = (mine[...].astype(F32), other[...].astype(F32))
    low = jnp.where(swap, b, a)
    high = jnp.where(swap, a, b)
    squares = jnp.sum(a * a + b * b)
    factor = jnp.minimum(1.0, limit * lax.rsqrt(jnp.full((1, a.shape[1]), squares, F32)))
    w = a.shape[1]
    full = (low * factor, high * factor)
    ef, eb, es, eg, nf, nb, ns, ng = outs
    half = 4 * w
    ef[...] = full[0][: 3 * w]
    es[...] = full[0][3 * w :]
    nf[...] = full[1][: 2 * w]
    ns[...] = full[1][2 * w : 3 * w]
    eb[...] = full[1][3 * w : 3 * w + 1]
    eg[...] = full[1][3 * w + 1 : 3 * w + 2]
    nb[...] = full[1][3 * w + 2 : 3 * w + 3]
    ng[...] = full[1][3 * w + 3 : 3 * w + 4]


VM = pl.BlockSpec(memory_space=pltpu.VMEM)
SM = pl.BlockSpec(memory_space=pltpu.SMEM)


def call(kernel, outs, scratch=(), specs=None, name=None):
    return pl.pallas_call(
        kernel,
        out_shape=outs,
        in_specs=specs,
        out_specs=jax.tree.map(lambda _: VM, outs),
        scratch_shapes=list(scratch),
        compiler_params=pltpu.CompilerParams(vmem_limit_bytes=VMEM_LIMIT),
        name=name,
    )


def flip(axis, bit):
    return [(i, i ^ bit) for i in range(lax.axis_size(axis))]


def pair_sum(parts):
    parts = [p.astype(F32) for p in parts]
    while len(parts) > 1:
        parts = [parts[i] + parts[i + 1] for i in range(0, len(parts), 2)]
    return parts[0].astype(BF)


def exchange(value, axis, bits):
    out = [value]
    for m in range(1, 1 << len(bits)):
        mask = sum(bits[j] for j in range(len(bits)) if m >> j & 1)
        out.append(lax.ppermute(value, axis, flip(axis, mask)))
    return out


def scatter_sum(value, axis, low, radix):
    spot = (lax.axis_index(axis) // low) % radix
    blocks = value.reshape((radix, value.shape[0] // radix) + value.shape[1:])
    got = []
    for k in range(radix):
        block = lax.dynamic_index_in_dim(blocks, spot ^ k, 0, False)
        got.append(block if k == 0 else lax.ppermute(block, axis, flip(axis, k * low)))
    return pair_sum(got)


def gather_back(value, axis, low, radix):
    spot = (lax.axis_index(axis) // low) % radix
    got = [value] + [lax.ppermute(value, axis, flip(axis, k * low)) for k in range(1, radix)]
    stack = jnp.stack(got)
    return jnp.concatenate(
        [lax.dynamic_index_in_dim(stack, spot ^ k, 0, False) for k in range(radix)], axis=0
    )


def reduce_rest(value):
    stream, cross = (lax.axis_size("stream"), lax.axis_size("cross"))
    value = scatter_sum(value, "stream", 2, 4)
    low = 8
    while low < stream:
        value = pair_sum(exchange(value, "stream", [low]))
        low *= 2
    low = 1
    while low < cross:
        value = pair_sum(exchange(value, "cross", [low, 2 * low] if 2 * low < cross else [low]))
        low *= 4
    return gather_back(value, "stream", 2, 4)


def shift(value, axis, step):
    size = lax.axis_size(axis)
    pairs = [(i, i + step) for i in range(size) if 0 <= i + step < size]
    return lax.ppermute(value, axis, pairs)


def per_device(
    latents,
    stale_latents,
    edge_latents,
    senders,
    receivers,
    edge_count,
    send_list,
    node_cotangent,
    edge_cotangent,
    edge_first,
    edge_bias,
    edge_second,
    edge_gain,
    node_first,
    node_bias,
    node_second,
    node_gain,
):
    n, w = latents.shape
    e = edge_latents.shape[0]
    depth = send_list.shape[2]
    lists = send_list[0]
    picked = call(
        pick_kernel, jax.ShapeDtypeStruct((4, depth, w), BF), specs=[VM, VM], name="pick"
    )(lists, stale_latents)
    halo = (
        shift(picked[0], "stream", 1),
        shift(picked[1], "stream", -1),
        shift(picked[2], "cross", 1),
        shift(picked[3], "cross", -1),
    )
    table = n + 4 * depth

    def shape(rows, kind=BF):
        return jax.ShapeDtypeStruct((rows, w), kind)

    new_latents, latent_grads, edge_grads, halo_grads, packed = call(
        main_kernel,
        (shape(n), shape(n), shape(e), shape(4 * depth), shape(8 * w)),
        scratch=(
            pltpu.VMEM((table, w), BF),
            pltpu.VMEM((e, n), BF),
            pltpu.VMEM((n, e), BF),
            pltpu.VMEM((table, e), BF),
            pltpu.VMEM((e, w), BF),
            pltpu.VMEM((e, w), BF),
            pltpu.VMEM((e, w), BF),
            pltpu.VMEM((e, w), F32),
            pltpu.VMEM((e, w), F32),
            pltpu.VMEM((e, w), F32),
            pltpu.VMEM((e, w), BF),
            pltpu.VMEM((e, w), BF),
            pltpu.VMEM((e, w), BF),
        ),
        specs=[SM] + [VM] * 18,
        name="layer",
    )(
        edge_count,
        latents,
        *halo,
        edge_latents,
        senders.reshape(e // w, w),
        receivers.reshape(e // w, w),
        node_cotangent,
        edge_cotangent,
        edge_first,
        edge_bias.reshape(1, w),
        edge_second,
        edge_gain.reshape(1, w),
        node_first,
        node_bias.reshape(1, w),
        node_second,
        node_gain.reshape(1, w),
    )
    back = halo_grads.reshape(4, depth, w)
    returned = (
        shift(back[0], "stream", -1),
        shift(back[1], "stream", 1),
        shift(back[2], "cross", -1),
        shift(back[3], "cross", 1),
    )
    stale_grads = call(stale_kernel, shape(n), specs=[VM] * 5, name="stale")(lists, *returned)

    bit = lax.axis_index("stream") % 2
    part = reduce_rest(scatter_sum(packed, "stream", 1, 2))
    other = lax.ppermute(part, "stream", flip("stream", 1))
    sizes = (3 * w * w, w, w * w, w, 2 * w * w, w, w * w, w)
    limit = math.sqrt(sum(sizes))
    clipped = call(
        functools.partial(final_kernel, limit),
        tuple(shape(s // w, F32) for s in sizes),
        specs=[SM, VM, VM],
        name="clip",
    )(bit.reshape(1), part, other)
    clipped = tuple(c.reshape(w) if s == w else c for c, s in zip(clipped, sizes))
    return (new_latents, latent_grads, stale_grads, edge_grads) + clipped


def solution(mesh):
    shard = P(("stream", "cross"))
    rows = P(("stream", "cross"), None)
    in_specs = (rows, rows, rows, shard, shard, shard, P(("stream", "cross"), None, None), rows, rows)
    in_specs = in_specs + (P(),) * 8
    out_specs = (rows,) * 4 + (P(),) * 8
    return jax.shard_map(
        per_device, mesh=mesh, in_specs=in_specs, out_specs=out_specs, check_vma=False
    )
```

time: 293 us -> 71.8 us (0.25)
  waiting for transfers between devices: 125 us -> 10.8 us
  other arithmetic: 55.3 us -> 0.11 us
  blocking collectives: 39.6 us -> 0 us
  between operations: 21 us -> 1.69 us
  starting transfers between devices: 24.8 us -> 38.4 us
  Pallas kernels: 0 us -> 12.9 us
  local copies, waits for them, and re-layouts: 17.7 us -> 6.74 us
  matrix products: 9 us -> 0 us
    psum x1 -> x0, waiting for transfers between devices: 122 us -> none  [per_device(): totals = lax.psum(grad_params, ('stream', 'cross'))]
    psum x1 -> x0, blocking collectives: 39.6 us -> none  [per_device(): totals = lax.psum(grad_params, ('stream', 'cross'))]
    scatter-add x4 -> x0, other arithmetic: 29.4 us -> none  [the longest x1 9.11 us: local_layer(): summed = jnp.zeros(owned.shape, jnp.float32).at[receivers].add(edge_alive...]
    ppermute x8 -> x19, starting transfers between devices: 24.7 us -> 38.4 us  [the longest x8 22.1 us: shift(): return lax.ppermute(value, axis, pairs)]
    pallas_call x0 -> x4, Pallas kernels: none -> 12.9 us  [the longest x1 10.6 us: per_device(): call(main_kernel, (shape(n), shape(n), shape(e), shape(4 * depth), shape(...]
    reduce_sum x13 -> x0, other arithmetic: 11.3 us -> none  [the longest x8 8.58 us: per_device(): squares = squares + jnp.sum(item * item)]
    gather x8 -> x0, local copies, waits for them, and re-layouts: 11.1 us -> none  [the longest x2 3.38 us: local_layer(): sender_rows = jnp.take(node_table, senders, axis=0)]
    dot_general x12 -> x0, matrix products: 9 us -> none  [the longest x3 3.03 us: local_layer(): jnp.dot(joined, edge_first, preferred_element_type=jnp.float32) + edge_bias]
  transfers between devices with their start and end apart: 9 -> 19, of which waited for: 2 -> 10; matrix products, arithmetic and copies ran while one was open for 8% -> 0% of each run, Pallas kernels for 0% -> 1%
where the time goes in v1:
time: 71.8 us; the launch traced here: 70.7 us
  starting transfers between devices  38.4 us (53%)
  Pallas kernels  12.9 us (18%)
  waiting for transfers between devices  10.8 us (15%)
  local copies, waits for them, and re-layouts  6.74 us (9%)
  between operations  1.69 us (2%)
    ppermute x8, starting transfers between devices, shift(): return lax.ppermute(value, axis, pairs)  22.1 us
    pallas_call x1, Pallas kernels, per_device(): call(main_kernel, (shape(n), shape(n), shape(e), shape(4 * depth), shape(...  10.6 us
    unnamed x34, local copies, waits for them, and re-layouts  6.68 us
    ppermute x1, starting transfers between devices, per_device(): other = lax.ppermute(part, 'stream', flip('stream', 1))  5.31 us
    ppermute x4, starting transfers between devices, scatter_sum(): lax.ppermute(block, axis, flip(axis, k * low))  4.63 us
    ppermute x4, waiting for transfers between devices, scatter_sum(): lax.ppermute(block, axis, flip(axis, k * low))  4.1 us
    ppermute x3, starting transfers between devices, exchange(): out.append(lax.ppermute(value, axis, flip(axis, mask)))  3.61 us
    ppermute x8, waiting for transfers between devices, shift(): return lax.ppermute(value, axis, pairs)  3.53 us
  transfers between devices with their start and end apart: 19, of which 10 were waited for; matrix products, arithmetic and copies ran while one was open for 0% of the time, Pallas kernels for 1%

profile of v1, /device:TPU:1, one launch (start us, length us, event | category | flops | bytes accessed | tf_op | source)
XLA Modules:
  0.0 70.7 jit_solution(16140762604648448823)
XLA Ops:
  0.7 0.9 %copy-done.2 = bf16[512,128]{1,0:T(8,128)(2,1)S(1)} copy-done((bf16[512,128]{1,0:T(8,128)(2,1)S(1)}, bf16[512,128]{1,0:T(8,128)(2,1)}, u32[]{:S(2)}) %copy-start.2) | copy-done | bytes 131096
  1.6 0.7 copy-done.11
  2.3 0.3 pick.1
  2.6 0.0 copy-start.3
  2.7 0.0 copy-start.7
  2.7 1.4 %collective-permute-start.3 = (bf16[128,128]{1,0:T(8,128)(2,1)S(1)}, bf16[128,128]{1,0:T(8,128)(2,1)S(1)}, u32[]{:S(2)}, u32[]{:S(2)}) collective-permute-start(bf16[128,128]{1,0:T(8,128)(2,1)S(1)} %get-tuple-element.49), channel_id=1, source_target_pairs={{1,0},{2,1},{3,2},{5,4},{6,5},{7,6},{9,8},{10,9},{11,10},{13,12},{... | collective-permute-start | bytes 98312 | tf_op jit(solution)/shard_map/ppermute | solution.py:315
  4.1 4.6 %collective-permute-start.2 = (bf16[128,128]{1,0:T(8,128)(2,1)S(1)}, bf16[128,128]{1,0:T(8,128)(2,1)S(1)}, u32[]{:S(2)}, u32[]{:S(2)}) collective-permute-start(bf16[128,128]{1,0:T(8,128)(2,1)S(1)} %get-tuple-element.50), channel_id=1, source_target_pairs={{0,1},{1,2},{2,3},{4,5},{5,6},{6,7},{8,9},{9,10},{10,11},{12,13},{... | collective-permute-start | bytes 98312 | tf_op jit(solution)/shard_map/ppermute | solution.py:315
  8.8 2.9 %collective-permute-start.1 = (bf16[128,128]{1,0:T(8,128)(2,1)S(1)}, bf16[128,128]{1,0:T(8,128)(2,1)S(1)}, u32[]{:S(2)}, u32[]{:S(2)}) collective-permute-start(bf16[128,128]{1,0:T(8,128)(2,1)S(1)} %get-tuple-element.51), channel_id=1, source_target_pairs={{4,0},{8,4},{12,8},{16,12},{20,16},{24,20},{28,24},{5,1},{9,5},{13... | collective-permute-start | bytes 98312 | tf_op jit(solution)/shard_map/ppermute | solution.py:315
  11.6 3.5 %collective-permute-start = (bf16[128,128]{1,0:T(8,128)(2,1)S(1)}, bf16[128,128]{1,0:T(8,128)(2,1)S(1)}, u32[]{:S(2)}, u32[]{:S(2)}) collective-permute-start(bf16[128,128]{1,0:T(8,128)(2,1)S(1)} %get-tuple-element.52), channel_id=1, source_target_pairs={{0,4},{4,8},{8,12},{12,16},{16,20},{20,24},{24,28},{1,5},{5,9},{9,... | collective-permute-start | bytes 98312 | tf_op jit(solution)/shard_map/ppermute | solution.py:315
  15.1 0.0 copy-start.15
  15.1 0.0 copy-start.16
  15.1 0.0 copy-start.10
  15.2 0.0 copy-start.9
  15.9 0.2 collective-permute-done.h0
  16.2 0.6 copy-done.13
  16.8 0.0 copy-done.14
  16.8 1.0 %copy-done.1 = bf16[1536,128]{1,0:T(8,128)(2,1)S(1)} copy-done((bf16[1536,128]{1,0:T(8,128)(2,1)S(1)}, bf16[1536,128]{1,0:T(8,128)(2,1)}, u32[]{:S(2)}) %copy-start.1) | copy-done | bytes 393240
  17.8 0.9 %copy-done.4 = bf16[512,128]{1,0:T(8,128)(2,1)S(1)} copy-done((bf16[512,128]{1,0:T(8,128)(2,1)S(1)}, bf16[512,128]{1,0:T(8,128)(2,1)}, u32[]{:S(2)}) %copy-start.4) | copy-done | bytes 131096
  18.7 0.9 %copy-done.5 = bf16[384,128]{1,0:T(8,128)(2,1)S(1)} copy-done((bf16[384,128]{1,0:T(8,128)(2,1)S(1)}, bf16[384,128]{1,0:T(8,128)(2,1)}, u32[]{:S(2)}) %copy-start.5) | copy-done | bytes 98328
  19.6 0.8 %copy-done.6 = bf16[256,128]{1,0:T(8,128)(2,1)S(1)} copy-done((bf16[256,128]{1,0:T(8,128)(2,1)S(1)}, bf16[256,128]{1,0:T(8,128)(2,1)}, u32[]{:S(2)}) %copy-start.6) | copy-done | bytes 65560
  20.4 0.8 %copy-done.8 = bf16[128,128]{1,0:T(8,128)(2,1)S(1)} copy-done((bf16[128,128]{1,0:T(8,128)(2,1)S(1)}, bf16[128,128]{1,0:T(8,128)(2,1)}, u32[]{:S(2)}) %copy-start.8) | copy-done | bytes 32792
  21.2 10.6 %layer.1 = (bf16[512,128]{1,0:T(8,128)(2,1)}, bf16[512,128]{1,0:T(8,128)(2,1)}, bf16[1536,128]{1,0:T(8,128)(2,1)}, bf16[512,128]{1,0:T(8,128)(2,1)S(1)}, bf16[1024,128]{1,0:T(8,128)(2,1)S(1)}) custom-call(s32[1]{0:T(128)S(6)} %copy.29.count_ref, bf16[512,128]{1,0:T(8,128)(2,1)S(1)} %copy-done.3, bf16[128,128]{1,0:T(8,128)(2,1)S(1)} %collective-permute-done.h0, ...), custom_call_target="tpu_custom_call" | custom-call | tf_op jit(solution)/shard_map/layer/pallas_call | solution.py:355
  31.8 0.1 collective-permute-start.8
  31.9 1.3 %collective-permute-done.8 = bf16[512,128]{1,0:T(8,128)(2,1)S(1)} collective-permute-done((bf16[512,128]{1,0:T(8,128)(2,1)S(1)}, bf16[512,128]{1,0:T(8,128)(2,1)S(1)}, u32[]{:S(2)}, u32[]{:S(2)}) %collective-permute-start.8) | collective-permute-done | bytes 131104 | tf_op jit(solution)/shard_map/ppermute | solution.py:285
  33.3 2.1 %collective-permute-start.9 = (bf16[128,128]{1,0:T(8,128)(2,1)S(1)}, bf16[128,128]{1,0:T(8,128)(2,1)S(1)}, u32[]{:S(2)}, u32[]{:S(2)}) collective-permute-start(bf16[128,128]{1,0:T(8,128)(2,1)S(1)} %get-tuple-element.42), channel_id=1, source_target_pairs={{0,8},{4,12},{8,0},{12,4},{16,24},{20,28},{24,16},{28,20},{1,9},{5... | collective-permute-start | bytes 98312 | tf_op jit(solution)/shard_map/ppermute | solution.py:285
  35.4 2.4 %collective-permute-start.11 = (bf16[128,128]{1,0:T(8,128)(2,1)S(1)}, bf16[128,128]{1,0:T(8,128)(2,1)S(1)}, u32[]{:S(2)}, u32[]{:S(2)}) collective-permute-start(bf16[128,128]{1,0:T(8,128)(2,1)S(1)} %get-tuple-element.43), channel_id=1, source_target_pairs={{0,24},{4,28},{8,16},{12,20},{16,8},{20,12},{24,0},{28,4},{1,25},{... | collective-permute-start | bytes 98312 | tf_op jit(solution)/shard_map/ppermute | solution.py:285
  37.8 1.6 %collective-permute-done.11 = bf16[128,128]{1,0:T(8,128)(2,1)S(1)} collective-permute-done((bf16[128,128]{1,0:T(8,128)(2,1)S(1)}, bf16[128,128]{1,0:T(8,128)(2,1)S(1)}, u32[]{:S(2)}, u32[]{:S(2)}) %collective-permute-start.11) | collective-permute-done | bytes 32800 | tf_op jit(solution)/shard_map/ppermute | solution.py:285
  39.5 1.2 %collective-permute-done.10 = bf16[128,128]{1,0:T(8,128)(2,1)S(1)} collective-permute-done((bf16[128,128]{1,0:T(8,128)(2,1)S(1)}, bf16[128,128]{1,0:T(8,128)(2,1)S(1)}, u32[]{:S(2)}, u32[]{:S(2)}) %collective-permute-start.10) | collective-permute-done | bytes 32800 | tf_op jit(solution)/shard_map/ppermute | solution.py:285
  40.7 1.5 %collective-permute-start.14 = (bf16[128,128]{1,0:T(8,128)(2,1)S(1)}, bf16[128,128]{1,0:T(8,128)(2,1)S(1)}, u32[]{:S(2)}, u32[]{:S(2)}) collective-permute-start(bf16[128,128]{1,0:T(8,128)(2,1)S(1)} %fusion.2), channel_id=1, source_target_pairs={{0,3},{1,2},{2,1},{3,0},{4,7},{5,6},{6,5},{7,4},{8,11},{9,10},{10,... | collective-permute-start | bytes 98312 | tf_op jit(solution)/shard_map/ppermute | solution.py:275
  42.1 1.1 %collective-permute-start.13 = (bf16[128,128]{1,0:T(8,128)(2,1)S(1)}, bf16[128,128]{1,0:T(8,128)(2,1)S(1)}, u32[]{:S(2)}, u32[]{:S(2)}) collective-permute-start(bf16[128,128]{1,0:T(8,128)(2,1)S(1)} %fusion.2), channel_id=1, source_target_pairs={{0,2},{1,3},{2,0},{3,1},{4,6},{5,7},{6,4},{7,5},{8,10},{9,11},{10,... | collective-permute-start | bytes 98312 | tf_op jit(solution)/shard_map/ppermute | solution.py:275
  43.2 1.1 %collective-permute-start.12 = (bf16[128,128]{1,0:T(8,128)(2,1)S(1)}, bf16[128,128]{1,0:T(8,128)(2,1)S(1)}, u32[]{:S(2)}, u32[]{:S(2)}) collective-permute-start(bf16[128,128]{1,0:T(8,128)(2,1)S(1)} %fusion.2), channel_id=1, source_target_pairs={{0,1},{1,0},{2,3},{3,2},{4,5},{5,4},{6,7},{7,6},{8,9},{9,8},{10,11... | collective-permute-start | bytes 98312 | tf_op jit(solution)/shard_map/ppermute | solution.py:275
  44.3 1.0 %collective-permute-done.14 = bf16[128,128]{1,0:T(8,128)(2,1)S(1)} collective-permute-done((bf16[128,128]{1,0:T(8,128)(2,1)S(1)}, bf16[128,128]{1,0:T(8,128)(2,1)S(1)}, u32[]{:S(2)}, u32[]{:S(2)}) %collective-permute-start.14) | collective-permute-done | bytes 32800 | tf_op jit(solution)/shard_map/ppermute | solution.py:275
  45.3 0.5 collective-permute-done.13
  45.8 0.3 collective-permute-done.12
  46.2 0.9 %collective-permute-start.17 = (bf16[128,128]{1,0:T(8,128)(2,1)S(1)}, bf16[128,128]{1,0:T(8,128)(2,1)S(1)}, u32[]{:S(2)}, u32[]{:S(2)}) collective-permute-start(bf16[128,128]{1,0:T(8,128)(2,1)S(1)} %add_convert_fusion), channel_id=1, source_target_pairs={{0,24},{4,28},{8,16},{12,20},{16,8},{20,12},{24,0},{28,4},{1,25},{... | collective-permute-start | bytes 98312 | tf_op jit(solution)/shard_map/ppermute | solution.py:291
  47.1 0.3 collective-permute-start.16
  47.4 1.4 %collective-permute-start.15 = (bf16[128,128]{1,0:T(8,128)(2,1)S(1)}, bf16[128,128]{1,0:T(8,128)(2,1)S(1)}, u32[]{:S(2)}, u32[]{:S(2)}) collective-permute-start(bf16[128,128]{1,0:T(8,128)(2,1)S(1)} %add_convert_fusion), channel_id=1, source_target_pairs={{0,8},{4,12},{8,0},{12,4},{16,24},{20,28},{24,16},{28,20},{1,9},{5... | collective-permute-start | bytes 98312 | tf_op jit(solution)/shard_map/ppermute | solution.py:291
  48.9 1.1 %collective-permute-done.17 = bf16[128,128]{1,0:T(8,128)(2,1)S(1)} collective-permute-done((bf16[128,128]{1,0:T(8,128)(2,1)S(1)}, bf16[128,128]{1,0:T(8,128)(2,1)S(1)}, u32[]{:S(2)}, u32[]{:S(2)}) %collective-permute-start.17) | collective-permute-done | bytes 32800 | tf_op jit(solution)/shard_map/ppermute | solution.py:291
  50.0 0.2 collective-permute-done.16
  50.3 5.3 %collective-permute-start.18 = (bf16[512,128]{1,0:T(8,128)(2,1)S(1)}, bf16[512,128]{1,0:T(8,128)(2,1)S(1)}, u32[]{:S(2)}, u32[]{:S(2)}) collective-permute-start(bf16[512,128]{1,0:T(8,128)(2,1)S(1)} %pad_maximum_fusion.1.mine), channel_id=1, source_target_pairs={{0,4},{4,0},{8,12},{12,8},{16,20},{20,16},{24,28},{28,24},{1,5},{5... | collective-permute-start | bytes 393224 | tf_op jit(solution)/shard_map/ppermute | solution.py:404
  55.6 3.0 %collective-permute-start.7 = (bf16[128,128]{1,0:T(8,128)(2,1)S(1)}, bf16[128,128]{1,0:T(8,128)(2,1)S(1)}, u32[]{:S(2)}, u32[]{:S(2)}) collective-permute-start(bf16[128,128]{1,0:T(8,128)(2,1)S(1)} %get-tuple-element.45), channel_id=1, source_target_pairs={{0,1},{1,2},{2,3},{4,5},{5,6},{6,7},{8,9},{9,10},{10,11},{12,13},{... | collective-permute-start | bytes 98312 | tf_op jit(solution)/shard_map/ppermute | solution.py:315
  58.6 0.0 copy-start.12
  58.6 1.3 %collective-permute-start.6 = (bf16[128,128]{1,0:T(8,128)(2,1)S(1)}, bf16[128,128]{1,0:T(8,128)(2,1)S(1)}, u32[]{:S(2)}, u32[]{:S(2)}) collective-permute-start(bf16[128,128]{1,0:T(8,128)(2,1)S(1)} %get-tuple-element.46), channel_id=1, source_target_pairs={{1,0},{2,1},{3,2},{5,4},{6,5},{7,6},{9,8},{10,9},{11,10},{13,12},{... | collective-permute-start | bytes 98312 | tf_op jit(solution)/shard_map/ppermute | solution.py:315
  59.9 3.5 %collective-permute-start.5 = (bf16[128,128]{1,0:T(8,128)(2,1)S(1)}, bf16[128,128]{1,0:T(8,128)(2,1)S(1)}, u32[]{:S(2)}, u32[]{:S(2)}) collective-permute-start(bf16[128,128]{1,0:T(8,128)(2,1)S(1)} %get-tuple-element.47), channel_id=1, source_target_pairs={{0,4},{4,8},{8,12},{12,16},{16,20},{20,24},{24,28},{1,5},{5,9},{9,... | collective-permute-start | bytes 98312 | tf_op jit(solution)/shard_map/ppermute | solution.py:315
  63.5 1.9 %collective-permute-start.4 = (bf16[128,128]{1,0:T(8,128)(2,1)S(1)}, bf16[128,128]{1,0:T(8,128)(2,1)S(1)}, u32[]{:S(2)}, u32[]{:S(2)}) collective-permute-start(bf16[128,128]{1,0:T(8,128)(2,1)S(1)} %get-tuple-element.48), channel_id=1, source_target_pairs={{4,0},{8,4},{12,8},{16,12},{20,16},{24,20},{28,24},{5,1},{9,5},{13... | collective-permute-start | bytes 98312 | tf_op jit(solution)/shard_map/ppermute | solution.py:315
  65.4 3.3 %collective-permute-done.4.b0 = bf16[128,128]{1,0:T(8,128)(2,1)S(1)} collective-permute-done((bf16[128,128]{1,0:T(8,128)(2,1)S(1)}, bf16[128,128]{1,0:T(8,128)(2,1)S(1)}, u32[]{:S(2)}, u32[]{:S(2)}) %collective-permute-start.4) | collective-permute-done | bytes 32800 | tf_op jit(solution)/shard_map/ppermute | solution.py:315
  68.7 1.0 %stale.1 = bf16[512,128]{1,0:T(8,128)(2,1)} custom-call(s32[4,128]{1,0:T(4,128)S(1)} %bitcast.53, bf16[128,128]{1,0:T(8,128)(2,1)S(1)} %collective-permute-done.4.b0, bf16[128,128]{1,0:T(8,128)(2,1)S(1)} %collective-permute-done.5.b1, bf16[128,128]{1,0:T(8,128)(2,1)S(1)} %collective-permute-done.6.b2, bf16[128,128]{1,0:T(8,128)(2,1)S(1)} %collective-permute-done.7.b3), custom_call_target="tpu_custom_call" | custom-call | tf_op jit(solution)/shard_map/stale/pallas_call | solution.py:400
  69.7 1.0 %clip.1 = (f32[384,128]{1,0:T(8,128)}, f32[1,128]{1,0:T(1,128)}, f32[128,128]{1,0:T(8,128)}, f32[1,128]{1,0:T(1,128)}, f32[256,128]{1,0:T(8,128)}, /*index=5*/f3...) custom-call(s32[1]{0:T(128)} %bitcast.11.bit_ref, bf16[512,128]{1,0:T(8,128)(2,1)S(1)} %pad_maximum_fusion.1.mine, ...), custom_call_target="tpu_custom_call" | custom-call | tf_op jit(solution)/shard_map/clip/pallas_call | solution.py:407
  (38 shorter events, 0.2 us)
Async XLA Ops:
  0.6 15.5 %copy-start = (bf16[1536,128]{1,0:T(8,128)(2,1)S(1)}, bf16[1536,128]{1,0:T(8,128)(2,1)}, u32[]{:S(2)}) copy-start(bf16[1536,128]{1,0:T(8,128)(2,1)} %edges.1) | copy-start | bytes 1179652
  0.7 1.0 %copy-start.2 = (bf16[512,128]{1,0:T(8,128)(2,1)S(1)}, bf16[512,128]{1,0:T(8,128)(2,1)}, u32[]{:S(2)}) copy-start(bf16[512,128]{1,0:T(8,128)(2,1)} %stale_ref.1) | copy-start | bytes 393220
  1.6 0.7 copy-start.11
  2.6 13.5 %copy-start.3 = (bf16[512,128]{1,0:T(8,128)(2,1)S(1)}, bf16[512,128]{1,0:T(8,128)(2,1)}, u32[]{:S(2)}) copy-start(bf16[512,128]{1,0:T(8,128)(2,1)} %latents.1) | copy-start | bytes 393220
  2.7 13.4 %copy-start.7 = (bf16[128,128]{1,0:T(8,128)(2,1)S(1)}, bf16[128,128]{1,0:T(8,128)(2,1)}, u32[]{:S(2)}) copy-start(bf16[128,128]{1,0:T(8,128)(2,1)} %edge_second.1) | copy-start | bytes 98308
  2.7 13.2 %collective-permute-start.3 = (bf16[128,128]{1,0:T(8,128)(2,1)S(1)}, bf16[128,128]{1,0:T(8,128)(2,1)S(1)}, u32[]{:S(2)}, u32[]{:S(2)}) collective-permute-start(bf16[128,128]{1,0:T(8,128)(2,1)S(1)} %get-tuple-element.49), channel_id=1, source_target_pairs={{1,0},{2,1},{3,2},{5,4},{6,5},{7,6},{9,8},{10,9},{11,10},{13,12},{... | collective-permute-start | bytes 98312 | tf_op jit(solution)/shard_map/ppermute | solution.py:315
  4.1 11.7 %collective-permute-start.2 = (bf16[128,128]{1,0:T(8,128)(2,1)S(1)}, bf16[128,128]{1,0:T(8,128)(2,1)S(1)}, u32[]{:S(2)}, u32[]{:S(2)}) collective-permute-start(bf16[128,128]{1,0:T(8,128)(2,1)S(1)} %get-tuple-element.50), channel_id=1, source_target_pairs={{0,1},{1,2},{2,3},{4,5},{5,6},{6,7},{8,9},{9,10},{10,11},{12,13},{... | collective-permute-start | bytes 98312 | tf_op jit(solution)/shard_map/ppermute | solution.py:315
  8.8 7.1 %collective-permute-start.1 = (bf16[128,128]{1,0:T(8,128)(2,1)S(1)}, bf16[128,128]{1,0:T(8,128)(2,1)S(1)}, u32[]{:S(2)}, u32[]{:S(2)}) collective-permute-start(bf16[128,128]{1,0:T(8,128)(2,1)S(1)} %get-tuple-element.51), channel_id=1, source_target_pairs={{4,0},{8,4},{12,8},{16,12},{20,16},{24,20},{28,24},{5,1},{9,5},{13... | collective-permute-start | bytes 98312 | tf_op jit(solution)/shard_map/ppermute | solution.py:315
  11.6 4.5 %collective-permute-start = (bf16[128,128]{1,0:T(8,128)(2,1)S(1)}, bf16[128,128]{1,0:T(8,128)(2,1)S(1)}, u32[]{:S(2)}, u32[]{:S(2)}) collective-permute-start(bf16[128,128]{1,0:T(8,128)(2,1)S(1)} %get-tuple-element.52), channel_id=1, source_target_pairs={{0,4},{4,8},{8,12},{12,16},{16,20},{20,24},{24,28},{1,5},{5,9},{9,... | collective-permute-start | bytes 98312 | tf_op jit(solution)/shard_map/ppermute | solution.py:315
  15.1 1.0 %copy-start.15 = (f32[128]{0:T(128)S(1)}, f32[128]{0:T(128)}, u32[]{:S(2)}) copy-start(f32[128]{0:T(128)} %param.31) | copy-start | bytes 1540
  15.1 1.0 %copy-start.16 = (f32[128]{0:T(128)S(1)}, f32[128]{0:T(128)}, u32[]{:S(2)}) copy-start(f32[128]{0:T(128)} %param.33) | copy-start | bytes 1540
  15.1 1.0 %copy-start.10 = (s32[1536]{0:T(1024)S(1)}, s32[1536]{0:T(1024)}, u32[]{:S(2)}) copy-start(s32[1536]{0:T(1024)} %param.21) | copy-start | bytes 18436
  15.2 1.0 %copy-start.9 = (s32[1536]{0:T(1024)S(1)}, s32[1536]{0:T(1024)}, u32[]{:S(2)}) copy-start(s32[1536]{0:T(1024)} %param.20) | copy-start | bytes 18436
  16.1 0.7 copy-start.13
  16.1 0.7 copy-start.14
  16.8 1.0 %copy-start.1 = (bf16[1536,128]{1,0:T(8,128)(2,1)S(1)}, bf16[1536,128]{1,0:T(8,128)(2,1)}, u32[]{:S(2)}) copy-start(bf16[1536,128]{1,0:T(8,128)(2,1)} %edge_cot.1) | copy-start | bytes 1179652
  17.8 0.9 %copy-start.4 = (bf16[512,128]{1,0:T(8,128)(2,1)S(1)}, bf16[512,128]{1,0:T(8,128)(2,1)}, u32[]{:S(2)}) copy-start(bf16[512,128]{1,0:T(8,128)(2,1)} %node_cot.1) | copy-start | bytes 393220
  18.7 0.9 %copy-start.5 = (bf16[384,128]{1,0:T(8,128)(2,1)S(1)}, bf16[384,128]{1,0:T(8,128)(2,1)}, u32[]{:S(2)}) copy-start(bf16[384,128]{1,0:T(8,128)(2,1)} %edge_first.1) | copy-start | bytes 294916
  19.6 0.8 %copy-start.6 = (bf16[256,128]{1,0:T(8,128)(2,1)S(1)}, bf16[256,128]{1,0:T(8,128)(2,1)}, u32[]{:S(2)}) copy-start(bf16[256,128]{1,0:T(8,128)(2,1)} %node_first.1) | copy-start | bytes 196612
  20.4 0.8 %copy-start.8 = (bf16[128,128]{1,0:T(8,128)(2,1)S(1)}, bf16[128,128]{1,0:T(8,128)(2,1)}, u32[]{:S(2)}) copy-start(bf16[128,128]{1,0:T(8,128)(2,1)} %node_second.1) | copy-start | bytes 98308
  31.8 1.4 %collective-permute-start.8 = (bf16[512,128]{1,0:T(8,128)(2,1)S(1)}, bf16[512,128]{1,0:T(8,128)(2,1)S(1)}, u32[]{:S(2)}, u32[]{:S(2)}) collective-permute-start(bf16[512,128]{1,0:T(8,128)(2,1)S(1)} %dynamic-slice_bitcast_fusion), channel_id=1, source_target_pairs={{0,4},{4,0},{8,12},{12,8},{16,20},{20,16},{24,28},{28,24},{1,5},{5... | collective-permute-start | bytes 393224 | tf_op jit(solution)/shard_map/ppermute | solution.py:285
  33.3 4.6 %collective-permute-start.9 = (bf16[128,128]{1,0:T(8,128)(2,1)S(1)}, bf16[128,128]{1,0:T(8,128)(2,1)S(1)}, u32[]{:S(2)}, u32[]{:S(2)}) collective-permute-start(bf16[128,128]{1,0:T(8,128)(2,1)S(1)} %get-tuple-element.42), channel_id=1, source_target_pairs={{0,8},{4,12},{8,0},{12,4},{16,24},{20,28},{24,16},{28,20},{1,9},{5... | collective-permute-start | bytes 98312 | tf_op jit(solution)/shard_map/ppermute | solution.py:285
  35.4 4.1 %collective-permute-start.11 = (bf16[128,128]{1,0:T(8,128)(2,1)S(1)}, bf16[128,128]{1,0:T(8,128)(2,1)S(1)}, u32[]{:S(2)}, u32[]{:S(2)}) collective-permute-start(bf16[128,128]{1,0:T(8,128)(2,1)S(1)} %get-tuple-element.43), channel_id=1, source_target_pairs={{0,24},{4,28},{8,16},{12,20},{16,8},{20,12},{24,0},{28,4},{1,25},{... | collective-permute-start | bytes 98312 | tf_op jit(solution)/shard_map/ppermute | solution.py:285
  37.8 2.8 %collective-permute-start.10 = (bf16[128,128]{1,0:T(8,128)(2,1)S(1)}, bf16[128,128]{1,0:T(8,128)(2,1)S(1)}, u32[]{:S(2)}, u32[]{:S(2)}) collective-permute-start(bf16[128,128]{1,0:T(8,128)(2,1)S(1)} %get-tuple-element.44), channel_id=1, source_target_pairs={{0,16},{4,20},{8,24},{12,28},{16,0},{20,4},{24,8},{28,12},{1,17},{... | collective-permute-start | bytes 98312 | tf_op jit(solution)/shard_map/ppermute | solution.py:285
  40.7 4.6 %collective-permute-start.14 = (bf16[128,128]{1,0:T(8,128)(2,1)S(1)}, bf16[128,128]{1,0:T(8,128)(2,1)S(1)}, u32[]{:S(2)}, u32[]{:S(2)}) collective-permute-start(bf16[128,128]{1,0:T(8,128)(2,1)S(1)} %fusion.2), channel_id=1, source_target_pairs={{0,3},{1,2},{2,1},{3,0},{4,7},{5,6},{6,5},{7,4},{8,11},{9,10},{10,... | collective-permute-start | bytes 98312 | tf_op jit(solution)/shard_map/ppermute | solution.py:275
  42.1 3.7 %collective-permute-start.13 = (bf16[128,128]{1,0:T(8,128)(2,1)S(1)}, bf16[128,128]{1,0:T(8,128)(2,1)S(1)}, u32[]{:S(2)}, u32[]{:S(2)}) collective-permute-start(bf16[128,128]{1,0:T(8,128)(2,1)S(1)} %fusion.2), channel_id=1, source_target_pairs={{0,2},{1,3},{2,0},{3,1},{4,6},{5,7},{6,4},{7,5},{8,10},{9,11},{10,... | collective-permute-start | bytes 98312 | tf_op jit(solution)/shard_map/ppermute | solution.py:275
  43.2 2.9 %collective-permute-start.12 = (bf16[128,128]{1,0:T(8,128)(2,1)S(1)}, bf16[128,128]{1,0:T(8,128)(2,1)S(1)}, u32[]{:S(2)}, u32[]{:S(2)}) collective-permute-start(bf16[128,128]{1,0:T(8,128)(2,1)S(1)} %fusion.2), channel_id=1, source_target_pairs={{0,1},{1,0},{2,3},{3,2},{4,5},{5,4},{6,7},{7,6},{8,9},{9,8},{10,11... | collective-permute-start | bytes 98312 | tf_op jit(solution)/shard_map/ppermute | solution.py:275
  46.2 3.8 %collective-permute-start.17 = (bf16[128,128]{1,0:T(8,128)(2,1)S(1)}, bf16[128,128]{1,0:T(8,128)(2,1)S(1)}, u32[]{:S(2)}, u32[]{:S(2)}) collective-permute-start(bf16[128,128]{1,0:T(8,128)(2,1)S(1)} %add_convert_fusion), channel_id=1, source_target_pairs={{0,24},{4,28},{8,16},{12,20},{16,8},{20,12},{24,0},{28,4},{1,25},{... | collective-permute-start | bytes 98312 | tf_op jit(solution)/shard_map/ppermute | solution.py:291
  47.1 3.1 %collective-permute-start.16 = (bf16[128,128]{1,0:T(8,128)(2,1)S(1)}, bf16[128,128]{1,0:T(8,128)(2,1)S(1)}, u32[]{:S(2)}, u32[]{:S(2)}) collective-permute-start(bf16[128,128]{1,0:T(8,128)(2,1)S(1)} %add_convert_fusion), channel_id=1, source_target_pairs={{0,16},{4,20},{8,24},{12,28},{16,0},{20,4},{24,8},{28,12},{1,17},{... | collective-permute-start | bytes 98312 | tf_op jit(solution)/shard_map/ppermute | solution.py:291
  47.4 2.8 %collective-permute-start.15 = (bf16[128,128]{1,0:T(8,128)(2,1)S(1)}, bf16[128,128]{1,0:T(8,128)(2,1)S(1)}, u32[]{:S(2)}, u32[]{:S(2)}) collective-permute-start(bf16[128,128]{1,0:T(8,128)(2,1)S(1)} %add_convert_fusion), channel_id=1, source_target_pairs={{0,8},{4,12},{8,0},{12,4},{16,24},{20,28},{24,16},{28,20},{1,9},{5... | collective-permute-start | bytes 98312 | tf_op jit(solution)/shard_map/ppermute | solution.py:291
  50.3 19.4 %collective-permute-start.18 = (bf16[512,128]{1,0:T(8,128)(2,1)S(1)}, bf16[512,128]{1,0:T(8,128)(2,1)S(1)}, u32[]{:S(2)}, u32[]{:S(2)}) collective-permute-start(bf16[512,128]{1,0:T(8,128)(2,1)S(1)} %pad_maximum_fusion.1.mine), channel_id=1, source_target_pairs={{0,4},{4,0},{8,12},{12,8},{16,20},{20,16},{24,28},{28,24},{1,5},{5... | collective-permute-start | bytes 393224 | tf_op jit(solution)/shard_map/ppermute | solution.py:404
  55.6 9.8 %collective-permute-start.7 = (bf16[128,128]{1,0:T(8,128)(2,1)S(1)}, bf16[128,128]{1,0:T(8,128)(2,1)S(1)}, u32[]{:S(2)}, u32[]{:S(2)}) collective-permute-start(bf16[128,128]{1,0:T(8,128)(2,1)S(1)} %get-tuple-element.45), channel_id=1, source_target_pairs={{0,1},{1,2},{2,3},{4,5},{5,6},{6,7},{8,9},{9,10},{10,11},{12,13},{... | collective-permute-start | bytes 98312 | tf_op jit(solution)/shard_map/ppermute | solution.py:315
  58.6 10.1 %copy-start.12 = (s32[1,4,128]{2,1,0:T(4,128)S(1)}, s32[1,4,128]{2,1,0:T(4,128)}, u32[]{:S(2)}) copy-start(s32[1,4,128]{2,1,0:T(4,128)} %param.23) | copy-start | bytes 6148
  58.6 6.8 %collective-permute-start.6 = (bf16[128,128]{1,0:T(8,128)(2,1)S(1)}, bf16[128,128]{1,0:T(8,128)(2,1)S(1)}, u32[]{:S(2)}, u32[]{:S(2)}) collective-permute-start(bf16[128,128]{1,0:T(8,128)(2,1)S(1)} %get-tuple-element.46), channel_id=1, source_target_pairs={{1,0},{2,1},{3,2},{5,4},{6,5},{7,6},{9,8},{10,9},{11,10},{13,12},{... | collective-permute-start | bytes 98312 | tf_op jit(solution)/shard_map/ppermute | solution.py:315
  59.9 5.5 %collective-permute-start.5 = (bf16[128,128]{1,0:T(8,128)(2,1)S(1)}, bf16[128,128]{1,0:T(8,128)(2,1)S(1)}, u32[]{:S(2)}, u32[]{:S(2)}) collective-permute-start(bf16[128,128]{1,0:T(8,128)(2,1)S(1)} %get-tuple-element.47), channel_id=1, source_target_pairs={{0,4},{4,8},{8,12},{12,16},{16,20},{20,24},{24,28},{1,5},{5,9},{9,... | collective-permute-start | bytes 98312 | tf_op jit(solution)/shard_map/ppermute | solution.py:315
  63.5 5.2 %collective-permute-start.4 = (bf16[128,128]{1,0:T(8,128)(2,1)S(1)}, bf16[128,128]{1,0:T(8,128)(2,1)S(1)}, u32[]{:S(2)}, u32[]{:S(2)}) collective-permute-start(bf16[128,128]{1,0:T(8,128)(2,1)S(1)} %get-tuple-element.48), channel_id=1, source_target_pairs={{4,0},{8,4},{12,8},{16,12},{20,16},{24,20},{28,24},{5,1},{9,5},{13... | collective-permute-start | bytes 98312 | tf_op jit(solution)/shard_map/ppermute | solution.py:315

commit v2 on v1

--- a/solution.py
+++ b/solution.py
@@ -27,7 +27,7 @@
 
 
 def index_columns(index_ref, row):
-    line = index_ref[row : row + 1, :].astype(F32)
+    line = index_ref[pl.ds(row, 1), :].astype(F32)
     return jnp.broadcast_to(line, (line.shape[1], line.shape[1])).T
 
 
@@ -42,23 +42,57 @@
 
 
 def one_hot_columns(index_ref, row, size):
-    line = index_ref[row : row + 1, :]
+    line = index_ref[pl.ds(row, 1), :]
     place = lax.broadcasted_iota(jnp.int32, (size, line.shape[1]), 0)
     return jnp.where(place == line, 1.0, 0.0).astype(BF)
 
 
-def pick_kernel(list_ref, stale_ref, out_ref):
-    width = list_ref.shape[1]
-    for block in range(list_ref.shape[0]):
-        hot = one_hot_rows(index_columns(list_ref, block), stale_ref.shape[0])
-        out_ref[block] = mm(hot, stale_ref[...]).astype(BF)
+def parities():
+    return (lax.rem(lax.axis_index("stream"), 2), lax.rem(lax.axis_index("cross"), 2))
+
+
+def inner(axis):
+    place = lax.axis_index(axis)
+    return jnp.logical_and(place > 0, place < lax.axis_size(axis) - 1)
+
+
+def list_order():
+    odd_s, odd_c = parities()
+    return (odd_s, 1 - odd_s, 2 + odd_c, 3 - odd_c)
+
+
+def load_kernel(list_hbm, stale_hbm, *rest):
+    count = (len(rest) - 4 - 3) // 2
+    sources = rest[:count]
+    outs = rest[count : count + 4]
+    kept = rest[count + 4 : 2 * count + 4]
+    lists, stale, sems = rest[2 * count + 4 :]
+    copies = [
+        pltpu.make_async_copy(a, b, sems.at[i])
+        for i, (a, b) in enumerate(
+            zip((list_hbm, stale_hbm) + sources, (lists, stale) + kept)
+        )
+    ]
+    for copy in copies:
+        copy.start()
+    copies[0].wait()
+    columns = [index_columns(lists, row) for row in list_order()]
+    copies[1].wait()
+    for column, out in zip(columns, outs):
+        out[...] = mm(one_hot_rows(column, stale.shape[0]), stale[...]).astype(BF)
+    for copy in copies[2:]:
+        copy.wait()
 
 
 def stale_kernel(list_ref, b0, b1, b2, b3, out_ref):
     total = None
-    for block, part in enumerate((b0, b1, b2, b3)):
-        hot = one_hot_columns(list_ref, block, out_ref.shape[0])
-        piece = mm(hot, part[...])
+    keep = (None, inner("stream"), None, inner("cross"))
+    for row, part, valid in zip(list_order(), (b0, b1, b2, b3), keep):
+        hot = one_hot_columns(list_ref, row, out_ref.shape[0])
+        part = part[...]
+        if valid is not None:
+            part = jnp.where(valid, part, jnp.zeros_like(part))
+        piece = mm(hot, part)
         total = piece if total is None else total + piece
     out_ref[...] = total.astype(BF)
 
@@ -106,7 +140,10 @@
     new_latents,
     latent_grads,
     edge_grads,
-    halo_grads,
+    g0,
+    g1,
+    g2,
+    g3,
     packed,
     table,
     hot_recv,
@@ -129,8 +166,18 @@
     total = count_ref[0]
     chunk = 2 * w
     table[:n] = latents[...]
-    for i, part in enumerate((h0, h1, h2, h3)):
-        table[n + i * depth : n + (i + 1) * depth] = part[...]
+    odd_s, odd_c = parities()
+    for i, (near, far, odd, axis) in enumerate(
+        ((h0, h1, odd_s, "stream"), (h2, h3, odd_c, "cross"))
+    ):
+        place = lax.axis_index(axis)
+        a, b = (near[...], far[...])
+        zero = jnp.zeros_like(a)
+        before = jnp.where(place > 0, jnp.where(odd == 1, a, b), zero)
+        after = jnp.where(place < lax.axis_size(axis) - 1, jnp.where(odd == 1, b, a), zero)
+        at = n + 2 * i * depth
+        table[at : at + depth] = before
+        table[at + depth : at + 2 * depth] = after
     gain = edge_gain[...]
 
     for c in range(e // chunk):
@@ -217,11 +264,16 @@
     latent_grads[...] = (
         latent_part + back[:n] + mm_nt(from_recv, edge_first[2 * w :])
     ).astype(BF)
-    halo_grads[...] = back[n:].astype(BF)
-
-
-def final_kernel(limit, bit_ref, mine, other, *outs):
-    swap = bit_ref[0] == 1
+    for i, (near, far, odd) in enumerate(((g0, g1, odd_s), (g2, g3, odd_c))):
+        at = n + 2 * i * depth
+        before = back[at : at + depth]
+        after = back[at + depth : at + 2 * depth]
+        near[...] = jnp.where(odd == 1, before, after).astype(BF)
+        far[...] = jnp.where(odd == 1, after, before).astype(BF)
+
+
+def final_kernel(limit, mine, other, *outs):
+    swap = half_of("stream") == 1
     a, b = (mine[...].astype(F32), other[...].astype(F32))
     low = jnp.where(swap, b, a)
     high = jnp.where(swap, a, b)
@@ -243,6 +295,7 @@
 
 VM = pl.BlockSpec(memory_space=pltpu.VMEM)
 SM = pl.BlockSpec(memory_space=pltpu.SMEM)
+HB = pl.BlockSpec(memory_space=pltpu.HBM)
 
 
 def call(kernel, outs, scratch=(), specs=None, name=None):
@@ -276,43 +329,80 @@
     return out
 
 
-def scatter_sum(value, axis, low, radix):
-    spot = (lax.axis_index(axis) // low) % radix
+def scatter_sum(value, axis, masks, spot):
+    radix = len(masks) + 1
     blocks = value.reshape((radix, value.shape[0] // radix) + value.shape[1:])
-    got = []
-    for k in range(radix):
-        block = lax.dynamic_index_in_dim(blocks, spot ^ k, 0, False)
-        got.append(block if k == 0 else lax.ppermute(block, axis, flip(axis, k * low)))
-    return pair_sum(got)
-
-
-def gather_back(value, axis, low, radix):
-    spot = (lax.axis_index(axis) // low) % radix
-    got = [value] + [lax.ppermute(value, axis, flip(axis, k * low)) for k in range(1, radix)]
-    stack = jnp.stack(got)
+    got = [lax.dynamic_index_in_dim(blocks, spot, 0, False)]
+    for k, mask in enumerate(masks):
+        block = lax.dynamic_index_in_dim(blocks, spot ^ (k + 1), 0, False)
+        got.append(lax.ppermute(block, axis, flip(axis, mask)))
+    return got
+
+
+def gather_back(value, axis, masks, spot):
+    stack = jnp.stack([value] + [lax.ppermute(value, axis, flip(axis, m)) for m in masks])
     return jnp.concatenate(
-        [lax.dynamic_index_in_dim(stack, spot ^ k, 0, False) for k in range(radix)], axis=0
-    )
-
-
-def reduce_rest(value):
+        [lax.dynamic_index_in_dim(stack, spot ^ k, 0, False) for k in range(len(masks) + 1)],
+        axis=0,
+    )
+
+
+QUAD = (3, 4, 7)
+
+
+def half_of(axis):
+    place = lax.axis_index(axis)
+    return lax.rem(place, 2) ^ lax.rem(place // 2, 2)
+
+
+def quarter_of(axis):
+    return lax.rem(lax.axis_index(axis) // 2, 4)
+
+
+def together(first, second):
+    return lax.optimization_barrier((tuple(first), tuple(second)))
+
+
+def odd_pairs(axis):
+    size = lax.axis_size(axis)
+    pairs = [(i, (i + 1) % size) for i in range(1, size, 2)]
+    return pairs + [(j, i) for i, j in pairs]
+
+
+def pair_exchange(near, far, axis):
+    return (
+        lax.ppermute(near, axis, flip(axis, 1)),
+        lax.ppermute(far, axis, odd_pairs(axis)),
+    )
+
+
+def reduce_all(value, near_s, far_s, near_c, far_c):
     stream, cross = (lax.axis_size("stream"), lax.axis_size("cross"))
-    value = scatter_sum(value, "stream", 2, 4)
+    half, quarter = (half_of("stream"), quarter_of("stream"))
+    parts, back_a = together(
+        scatter_sum(value, "stream", (1,), half),
+        (lax.ppermute(near_s, "stream", flip("stream", 1)),),
+    )
+    value = pair_sum(parts)
+    parts, back_c = together(
+        scatter_sum(value, "stream", QUAD, quarter), pair_exchange(near_c, far_c, "cross")
+    )
+    value = pair_sum(parts)
     low = 8
     while low < stream:
         value = pair_sum(exchange(value, "stream", [low]))
         low *= 2
-    low = 1
+    parts, back_b = together(
+        exchange(value, "cross", [1, 2]),
+        (lax.ppermute(far_s, "stream", odd_pairs("stream")),),
+    )
+    value = pair_sum(parts)
+    low = 4
     while low < cross:
         value = pair_sum(exchange(value, "cross", [low, 2 * low] if 2 * low < cross else [low]))
         low *= 4
-    return gather_back(value, "stream", 2, 4)
-
-
-def shift(value, axis, step):
-    size = lax.axis_size(axis)
-    pairs = [(i, i + step) for i in range(size) if 0 <= i + step < size]
-    return lax.ppermute(value, axis, pairs)
+    value = gather_back(value, "stream", QUAD, quarter)
+    return (value, back_a + back_b + back_c)
 
 
 def per_device(
@@ -338,23 +428,46 @@
     e = edge_latents.shape[0]
     depth = send_list.shape[2]
     lists = send_list[0]
-    picked = call(
-        pick_kernel, jax.ShapeDtypeStruct((4, depth, w), BF), specs=[VM, VM], name="pick"
-    )(lists, stale_latents)
-    halo = (
-        shift(picked[0], "stream", 1),
-        shift(picked[1], "stream", -1),
-        shift(picked[2], "cross", 1),
-        shift(picked[3], "cross", -1),
-    )
+
+    sources = (
+        latents,
+        edge_latents,
+        senders.reshape(e // w, w),
+        receivers.reshape(e // w, w),
+        node_cotangent,
+        edge_cotangent,
+        edge_first,
+        edge_bias.reshape(1, w),
+        edge_second,
+        edge_gain.reshape(1, w),
+        node_first,
+        node_bias.reshape(1, w),
+        node_second,
+        node_gain.reshape(1, w),
+    )
+    loaded = call(
+        load_kernel,
+        (jax.ShapeDtypeStruct((depth, w), BF),) * 4
+        + tuple(jax.ShapeDtypeStruct(x.shape, x.dtype) for x in sources),
+        scratch=(
+            pltpu.VMEM(lists.shape, lists.dtype),
+            pltpu.VMEM((n, w), BF),
+            pltpu.SemaphoreType.DMA((2 + len(sources),)),
+        ),
+        specs=[HB] * (2 + len(sources)),
+        name="load",
+    )(*(pltpu.with_memory_space_constraint(x, pltpu.HBM) for x in (lists, stale_latents) + sources))
+    picked, kept = (loaded[:4], loaded[4:])
+    halo = pair_exchange(picked[2], picked[3], "cross")
+    halo = pair_exchange(picked[0], picked[1], "stream") + halo
     table = n + 4 * depth
 
     def shape(rows, kind=BF):
         return jax.ShapeDtypeStruct((rows, w), kind)
 
-    new_latents, latent_grads, edge_grads, halo_grads, packed = call(
+    new_latents, latent_grads, edge_grads, g0, g1, g2, g3, packed = call(
         main_kernel,
-        (shape(n), shape(n), shape(e), shape(4 * depth), shape(8 * w)),
+        (shape(n), shape(n), shape(e)) + (shape(depth),) * 4 + (shape(8 * w),),
         scratch=(
             pltpu.VMEM((table, w), BF),
             pltpu.VMEM((e, n), BF),
@@ -373,43 +486,19 @@
         specs=[SM] + [VM] * 18,
         name="layer",
     )(
-        edge_count,
-        latents,
-        *halo,
-        edge_latents,
-        senders.reshape(e // w, w),
-        receivers.reshape(e // w, w),
-        node_cotangent,
-        edge_cotangent,
-        edge_first,
-        edge_bias.reshape(1, w),
-        edge_second,
-        edge_gain.reshape(1, w),
-        node_first,
-        node_bias.reshape(1, w),
-        node_second,
-        node_gain.reshape(1, w),
-    )
-    back = halo_grads.reshape(4, depth, w)
-    returned = (
-        shift(back[0], "stream", -1),
-        shift(back[1], "stream", 1),
-        shift(back[2], "cross", -1),
-        shift(back[3], "cross", 1),
-    )
+        edge_count, kept[0], *halo, *kept[1:]
+    )
+    part, returned = reduce_all(packed, g0, g1, g2, g3)
     stale_grads = call(stale_kernel, shape(n), specs=[VM] * 5, name="stale")(lists, *returned)
-
-    bit = lax.axis_index("stream") % 2
-    part = reduce_rest(scatter_sum(packed, "stream", 1, 2))
     other = lax.ppermute(part, "stream", flip("stream", 1))
     sizes = (3 * w * w, w, w * w, w, 2 * w * w, w, w * w, w)
     limit = math.sqrt(sum(sizes))
     clipped = call(
         functools.partial(final_kernel, limit),
         tuple(shape(s // w, F32) for s in sizes),
-        specs=[SM, VM, VM],
+        specs=[VM, VM],
         name="clip",
-    )(bit.reshape(1), part, other)
+    )(part, other)
     clipped = tuple(c.reshape(w) if s == w else c for c, s in zip(clipped, sizes))
     return (new_latents, latent_grads, stale_grads, edge_grads) + clipped
 

time: 71.8 us -> 49.5 us (0.69); the launches traced: 70.7 us -> 49.3 us
  starting transfers between devices: 38.4 us -> 23 us
  local copies, waits for them, and re-layouts: 6.74 us -> 0.64 us
  Pallas kernels: 12.9 us -> 14.1 us
  waiting for transfers between devices: 10.8 us -> 9.96 us
    ppermute x15, starting transfers between devices: 29.5 us -> 19 us  [the longest x3 7.04 us: pair_exchange(): lax.ppermute(far, axis, odd_pairs(axis))]
    unnamed x34 -> x2, local copies, waits for them, and re-layouts: 6.68 us -> 0.58 us
    ppermute x1, starting transfers between devices: 5.31 us -> 0.07 us  [per_device(): other = lax.ppermute(part, 'stream', flip('stream', 1))]
    ppermute x15, waiting for transfers between devices: 8.95 us -> 7.56 us  [the longest x3 3.71 us: gather_back(): lax.ppermute(value, axis, flip(axis, m))]
    pallas_call x2, Pallas kernels: 10.9 us -> 12.1 us  [the longest x1 10.6 us: per_device(): call(main_kernel, (shape(n), shape(n), shape(e)) + (shape(depth),) * 4 +...]
  transfers between devices with their start and end apart: 19 -> 19, of which waited for: 10 -> 8; matrix products, arithmetic and copies ran while one was open for 0% -> 0% of each run, Pallas kernels for 1% -> 2%
where the time goes in v2:
time: 49.5 us; the launch traced here: 49.3 us
  starting transfers between devices  23 us (46%)
  Pallas kernels  14.1 us (28%)
  waiting for transfers between devices  9.96 us (20%)
  between operations  1.42 us (3%)
  local copies, waits for them, and re-layouts  0.64 us (1%)
    pallas_call x1, Pallas kernels, per_device(): call(main_kernel, (shape(n), shape(n), shape(e)) + (shape(depth),) * 4 +...  10.6 us
    ppermute x3, starting transfers between devices, pair_exchange(): lax.ppermute(far, axis, odd_pairs(axis))  7.04 us
    ppermute x4, starting transfers between devices, scatter_sum(): got.append(lax.ppermute(block, axis, flip(axis, mask)))  6.15 us
    ppermute x3, starting transfers between devices, gather_back(): lax.ppermute(value, axis, flip(axis, m))  4.33 us
    ppermute x3, starting transfers between devices, exchange(): out.append(lax.ppermute(value, axis, flip(axis, mask)))  3.96 us
    ppermute x3, waiting for transfers between devices, gather_back(): lax.ppermute(value, axis, flip(axis, m))  3.71 us
    ppermute x3, waiting for transfers between devices, exchange(): out.append(lax.ppermute(value, axis, flip(axis, mask)))  2.4 us
    ppermute x4, waiting for transfers between devices, scatter_sum(): got.append(lax.ppermute(block, axis, flip(axis, mask)))  2.15 us
  transfers between devices with their start and end apart: 19, of which 8 were waited for; matrix products, arithmetic and copies ran while one was open for 0% of the time, Pallas kernels for 2%

profile of v2, /device:TPU:1, one launch (start us, length us, event | category | flops | bytes accessed | tf_op | source)
XLA Modules:
  0.0 49.3 jit_solution(4946420957790733260)
XLA Ops:
  0.7 1.5 %load.1 = (bf16[128,128]{1,0:T(8,128)(2,1)S(1)}, bf16[128,128]{1,0:T(8,128)(2,1)S(1)}, bf16[128,128]{1,0:T(8,128)(2,1)S(1)}, bf16[128,128]{1,0:T(8,128)(2,1)S(1)...) custom-call(s32[4,128]{1,0:T(4,128)} %bitcast.38, ...), custom_call_target="tpu_custom_call" | custom-call | tf_op jit(solution)/shard_map/load/pallas_call | solution.py:448
  2.2 0.1 collective-permute-start
  2.3 2.7 %collective-permute-start.1 = (bf16[128,128]{1,0:T(8,128)(2,1)S(1)}, bf16[128,128]{1,0:T(8,128)(2,1)S(1)}, u32[]{:S(2)}, u32[]{:S(2)}) collective-permute-start(bf16[128,128]{1,0:T(8,128)(2,1)S(1)} %get-tuple-element.62), channel_id=1, source_target_pairs={{4,8},{12,16},{20,24},{28,0},{8,4},{16,12},{24,20},{0,28},{5,9},{1... | collective-permute-start | bytes 98312 | tf_op jit(solution)/shard_map/ppermute | solution.py:375
  4.9 1.3 %collective-permute-start.2 = (bf16[128,128]{1,0:T(8,128)(2,1)S(1)}, bf16[128,128]{1,0:T(8,128)(2,1)S(1)}, u32[]{:S(2)}, u32[]{:S(2)}) collective-permute-start(bf16[128,128]{1,0:T(8,128)(2,1)S(1)} %get-tuple-element.63), channel_id=1, source_target_pairs={{0,1},{1,0},{2,3},{3,2},{4,5},{5,4},{6,7},{7,6},{8,9},{9,8},{10,11... | collective-permute-start | bytes 98312 | tf_op jit(solution)/shard_map/ppermute | solution.py:374
  6.2 2.2 %collective-permute-start.3 = (bf16[128,128]{1,0:T(8,128)(2,1)S(1)}, bf16[128,128]{1,0:T(8,128)(2,1)S(1)}, u32[]{:S(2)}, u32[]{:S(2)}) collective-permute-start(bf16[128,128]{1,0:T(8,128)(2,1)S(1)} %get-tuple-element.64), channel_id=1, source_target_pairs={{1,2},{3,0},{2,1},{0,3},{5,6},{7,4},{6,5},{4,7},{9,10},{11,8},{10,... | collective-permute-start | bytes 98312 | tf_op jit(solution)/shard_map/ppermute | solution.py:375
  9.1 0.0 collective-permute-done.h0
  9.1 0.0 collective-permute-done.1.h1
  9.1 0.0 collective-permute-done.2.h2
  9.1 1.7 %collective-permute-done.3.h3 = bf16[128,128]{1,0:T(8,128)(2,1)S(1)} collective-permute-done((bf16[128,128]{1,0:T(8,128)(2,1)S(1)}, bf16[128,128]{1,0:T(8,128)(2,1)S(1)}, u32[]{:S(2)}, u32[]{:S(2)}) %collective-permute-start.3) | collective-permute-done | bytes 32800 | tf_op jit(solution)/shard_map/ppermute | solution.py:375
  10.8 10.6 %layer.1 = (bf16[512,128]{1,0:T(8,128)(2,1)}, bf16[512,128]{1,0:T(8,128)(2,1)}, bf16[1536,128]{1,0:T(8,128)(2,1)}, bf16[128,128]{1,0:T(8,128)(2,1)S(1)}, bf16[12...) custom-call(s32[1]{0:T(128)S(6)} %copy.29.count_ref, ...), custom_call_target="tpu_custom_call" | custom-call | tf_op jit(solution)/shard_map/layer/pallas_call | solution.py:468
  21.4 2.9 %collective-permute-start.4 = (bf16[512,128]{1,0:T(8,128)(2,1)S(1)}, bf16[512,128]{1,0:T(8,128)(2,1)S(1)}, u32[]{:S(2)}, u32[]{:S(2)}) collective-permute-start(bf16[512,128]{1,0:T(8,128)(2,1)S(1)} %get-tuple-element.108), channel_id=1, source_target_pairs={{0,4},{4,0},{8,12},{12,8},{16,20},{20,16},{24,28},{28,24},{1,5},{5... | collective-permute-start | bytes 393224 | tf_op jit(solution)/shard_map/ppermute | solution.py:338
  24.3 0.1 collective-permute-start.5
  24.4 2.2 %collective-permute-start.10 = (bf16[128,128]{1,0:T(8,128)(2,1)S(1)}, bf16[128,128]{1,0:T(8,128)(2,1)S(1)}, u32[]{:S(2)}, u32[]{:S(2)}) collective-permute-start(bf16[128,128]{1,0:T(8,128)(2,1)S(1)} %get-tuple-element.86), channel_id=1, source_target_pairs={{1,2},{3,0},{2,1},{0,3},{5,6},{7,4},{6,5},{4,7},{9,10},{11,8},{10,... | collective-permute-start | bytes 98312 | tf_op jit(solution)/shard_map/ppermute | solution.py:375
  26.6 0.0 collective-permute-start.9
  26.6 0.0 collective-permute-done.5.b0
  26.6 0.0 collective-permute-done.4
  26.6 0.1 collective-permute-start.6
  26.7 1.1 %collective-permute-start.7 = (bf16[128,128]{1,0:T(8,128)(2,1)S(1)}, bf16[128,128]{1,0:T(8,128)(2,1)S(1)}, u32[]{:S(2)}, u32[]{:S(2)}) collective-permute-start(bf16[128,128]{1,0:T(8,128)(2,1)S(1)} %get-tuple-element.115), channel_id=1, source_target_pairs={{0,16},{4,20},{8,24},{12,28},{16,0},{20,4},{24,8},{28,12},{1,17},{... | collective-permute-start | bytes 98312 | tf_op jit(solution)/shard_map/ppermute | solution.py:338
  27.8 2.1 %collective-permute-start.8 = (bf16[128,128]{1,0:T(8,128)(2,1)S(1)}, bf16[128,128]{1,0:T(8,128)(2,1)S(1)}, u32[]{:S(2)}, u32[]{:S(2)}) collective-permute-start(bf16[128,128]{1,0:T(8,128)(2,1)S(1)} %get-tuple-element.114), channel_id=1, source_target_pairs={{0,28},{4,24},{8,20},{12,16},{16,12},{20,8},{24,4},{28,0},{1,29},{... | collective-permute-start | bytes 98312 | tf_op jit(solution)/shard_map/ppermute | solution.py:338
  29.9 0.0 collective-permute-done.10.b3
  29.9 0.0 collective-permute-start.14
  29.9 0.0 collective-permute-done.9.b2
  29.9 0.7 %collective-permute-done.6 = bf16[128,128]{1,0:T(8,128)(2,1)S(1)} collective-permute-done((bf16[128,128]{1,0:T(8,128)(2,1)S(1)}, bf16[128,128]{1,0:T(8,128)(2,1)S(1)}, u32[]{:S(2)}, u32[]{:S(2)}) %collective-permute-start.6) | collective-permute-done | bytes 32800 | tf_op jit(solution)/shard_map/ppermute | solution.py:338
  30.7 0.0 collective-permute-done.7
  30.7 1.4 %collective-permute-done.8 = bf16[128,128]{1,0:T(8,128)(2,1)S(1)} collective-permute-done((bf16[128,128]{1,0:T(8,128)(2,1)S(1)}, bf16[128,128]{1,0:T(8,128)(2,1)S(1)}, u32[]{:S(2)}, u32[]{:S(2)}) %collective-permute-start.8) | collective-permute-done | bytes 32800 | tf_op jit(solution)/shard_map/ppermute | solution.py:338
  32.1 1.8 %collective-permute-start.11 = (bf16[128,128]{1,0:T(8,128)(2,1)S(1)}, bf16[128,128]{1,0:T(8,128)(2,1)S(1)}, u32[]{:S(2)}, u32[]{:S(2)}) collective-permute-start(bf16[128,128]{1,0:T(8,128)(2,1)S(1)} %add_convert_fusion.2), channel_id=1, source_target_pairs={{0,1},{1,0},{2,3},{3,2},{4,5},{5,4},{6,7},{7,6},{8,9},{9,8},{10,11... | collective-permute-start | bytes 98312 | tf_op jit(solution)/shard_map/ppermute | solution.py:328
  33.9 0.0 collective-permute-start.12
  33.9 2.2 %collective-permute-start.13 = (bf16[128,128]{1,0:T(8,128)(2,1)S(1)}, bf16[128,128]{1,0:T(8,128)(2,1)S(1)}, u32[]{:S(2)}, u32[]{:S(2)}) collective-permute-start(bf16[128,128]{1,0:T(8,128)(2,1)S(1)} %add_convert_fusion.2), channel_id=1, source_target_pairs={{0,3},{1,2},{2,1},{3,0},{4,7},{5,6},{6,5},{7,4},{8,11},{9,10},{10,... | collective-permute-start | bytes 98312 | tf_op jit(solution)/shard_map/ppermute | solution.py:328
  36.1 0.0 collective-permute-done.14.b1
  36.1 0.0 collective-permute-done.11
  36.1 2.0 %collective-permute-done.12 = bf16[128,128]{1,0:T(8,128)(2,1)S(1)} collective-permute-done((bf16[128,128]{1,0:T(8,128)(2,1)S(1)}, bf16[128,128]{1,0:T(8,128)(2,1)S(1)}, u32[]{:S(2)}, u32[]{:S(2)}) %collective-permute-start.12) | collective-permute-done | bytes 32800 | tf_op jit(solution)/shard_map/ppermute | solution.py:328
  38.1 0.4 collective-permute-done.13
  38.5 2.8 %collective-permute-start.15 = (bf16[128,128]{1,0:T(8,128)(2,1)S(1)}, bf16[128,128]{1,0:T(8,128)(2,1)S(1)}, u32[]{:S(2)}, u32[]{:S(2)}) collective-permute-start(bf16[128,128]{1,0:T(8,128)(2,1)S(1)} %add_convert_fusion.1), channel_id=1, source_target_pairs={{0,12},{4,8},{8,4},{12,0},{16,28},{20,24},{24,20},{28,16},{1,13},{... | collective-permute-start | bytes 98312 | tf_op jit(solution)/shard_map/ppermute | solution.py:343
  41.3 1.0 %collective-permute-start.16 = (bf16[128,128]{1,0:T(8,128)(2,1)S(1)}, bf16[128,128]{1,0:T(8,128)(2,1)S(1)}, u32[]{:S(2)}, u32[]{:S(2)}) collective-permute-start(bf16[128,128]{1,0:T(8,128)(2,1)S(1)} %add_convert_fusion.1), channel_id=1, source_target_pairs={{0,16},{4,20},{8,24},{12,28},{16,0},{20,4},{24,8},{28,12},{1,17},{... | collective-permute-start | bytes 98312 | tf_op jit(solution)/shard_map/ppermute | solution.py:343
  42.3 0.5 %collective-permute-start.17 = (bf16[128,128]{1,0:T(8,128)(2,1)S(1)}, bf16[128,128]{1,0:T(8,128)(2,1)S(1)}, u32[]{:S(2)}, u32[]{:S(2)}) collective-permute-start(bf16[128,128]{1,0:T(8,128)(2,1)S(1)} %add_convert_fusion.1), channel_id=1, source_target_pairs={{0,28},{4,24},{8,20},{12,16},{16,12},{20,8},{24,4},{28,0},{1,29},{... | collective-permute-start | bytes 98312 | tf_op jit(solution)/shard_map/ppermute | solution.py:343
  42.8 0.7 %collective-permute-done.15 = bf16[128,128]{1,0:T(8,128)(2,1)S(1)} collective-permute-done((bf16[128,128]{1,0:T(8,128)(2,1)S(1)}, bf16[128,128]{1,0:T(8,128)(2,1)S(1)}, u32[]{:S(2)}, u32[]{:S(2)}) %collective-permute-start.15) | collective-permute-done | bytes 32800 | tf_op jit(solution)/shard_map/ppermute | solution.py:343
  43.5 0.5 %collective-permute-done.16 = bf16[128,128]{1,0:T(8,128)(2,1)S(1)} collective-permute-done((bf16[128,128]{1,0:T(8,128)(2,1)S(1)}, bf16[128,128]{1,0:T(8,128)(2,1)S(1)}, u32[]{:S(2)}, u32[]{:S(2)}) %collective-permute-start.16) | collective-permute-done | bytes 32800 | tf_op jit(solution)/shard_map/ppermute | solution.py:343
  44.1 2.5 %collective-permute-done.17 = bf16[128,128]{1,0:T(8,128)(2,1)S(1)} collective-permute-done((bf16[128,128]{1,0:T(8,128)(2,1)S(1)}, bf16[128,128]{1,0:T(8,128)(2,1)S(1)}, u32[]{:S(2)}, u32[]{:S(2)}) %collective-permute-start.17) | collective-permute-done | bytes 32800 | tf_op jit(solution)/shard_map/ppermute | solution.py:343
  46.6 0.0 copy-start
  46.6 0.1 collective-permute-start.18
  46.7 0.6 %copy-done = s32[1,4,128]{2,1,0:T(4,128)S(1)} copy-done((s32[1,4,128]{2,1,0:T(4,128)S(1)}, s32[1,4,128]{2,1,0:T(4,128)}, u32[]{:S(2)}) %copy-start) | copy-done | bytes 2072
  47.3 1.0 %stale.1 = bf16[512,128]{1,0:T(8,128)(2,1)} custom-call(s32[4,128]{1,0:T(4,128)S(1)} %bitcast.39, bf16[128,128]{1,0:T(8,128)(2,1)S(1)} %collective-permute-done.5.b0, bf16[128,128]{1,0:T(8,128)(2,1)S(1)} %collective-permute-done.14.b1, bf16[128,128]{1,0:T(8,128)(2,1)S(1)} %collective-permute-done.9.b2, bf16[128,128]{1,0:T(8,128)(2,1)S(1)} %collective-permute-done.10.b3), custom_call_target="tpu_custom_call" | custom-call | tf_op jit(solution)/shard_map/stale/pallas_call | solution.py:492
  48.2 0.0 collective-permute-done.18.other
  48.2 1.0 %clip.1 = (f32[384,128]{1,0:T(8,128)}, f32[1,128]{1,0:T(1,128)}, f32[128,128]{1,0:T(8,128)}, f32[1,128]{1,0:T(1,128)}, f32[256,128]{1,0:T(8,128)}, /*index=5*/f3...) custom-call(bf16[512,128]{1,0:T(8,128)(2,1)S(1)} %pad_maximum_fusion.1.mine, ...), custom_call_target="tpu_custom_call" | custom-call | tf_op jit(solution)/shard_map/clip/pallas_call | solution.py:496
  (8 shorter events, 0.2 us)
Async XLA Ops:
  2.2 6.9 %collective-permute-start = (bf16[128,128]{1,0:T(8,128)(2,1)S(1)}, bf16[128,128]{1,0:T(8,128)(2,1)S(1)}, u32[]{:S(2)}, u32[]{:S(2)}) collective-permute-start(bf16[128,128]{1,0:T(8,128)(2,1)S(1)} %get-tuple-element.61), channel_id=1, source_target_pairs={{0,4},{4,0},{8,12},{12,8},{16,20},{20,16},{24,28},{28,24},{1,5},{5... | collective-permute-start | bytes 98312 | tf_op jit(solution)/shard_map/ppermute | solution.py:374
  2.3 6.8 %collective-permute-start.1 = (bf16[128,128]{1,0:T(8,128)(2,1)S(1)}, bf16[128,128]{1,0:T(8,128)(2,1)S(1)}, u32[]{:S(2)}, u32[]{:S(2)}) collective-permute-start(bf16[128,128]{1,0:T(8,128)(2,1)S(1)} %get-tuple-element.62), channel_id=1, source_target_pairs={{4,8},{12,16},{20,24},{28,0},{8,4},{16,12},{24,20},{0,28},{5,9},{1... | collective-permute-start | bytes 98312 | tf_op jit(solution)/shard_map/ppermute | solution.py:375
  4.9 4.2 %collective-permute-start.2 = (bf16[128,128]{1,0:T(8,128)(2,1)S(1)}, bf16[128,128]{1,0:T(8,128)(2,1)S(1)}, u32[]{:S(2)}, u32[]{:S(2)}) collective-permute-start(bf16[128,128]{1,0:T(8,128)(2,1)S(1)} %get-tuple-element.63), channel_id=1, source_target_pairs={{0,1},{1,0},{2,3},{3,2},{4,5},{5,4},{6,7},{7,6},{8,9},{9,8},{10,11... | collective-permute-start | bytes 98312 | tf_op jit(solution)/shard_map/ppermute | solution.py:374
  6.2 4.6 %collective-permute-start.3 = (bf16[128,128]{1,0:T(8,128)(2,1)S(1)}, bf16[128,128]{1,0:T(8,128)(2,1)S(1)}, u32[]{:S(2)}, u32[]{:S(2)}) collective-permute-start(bf16[128,128]{1,0:T(8,128)(2,1)S(1)} %get-tuple-element.64), channel_id=1, source_target_pairs={{1,2},{3,0},{2,1},{0,3},{5,6},{7,4},{6,5},{4,7},{9,10},{11,8},{10,... | collective-permute-start | bytes 98312 | tf_op jit(solution)/shard_map/ppermute | solution.py:375
  21.4 5.2 %collective-permute-start.4 = (bf16[512,128]{1,0:T(8,128)(2,1)S(1)}, bf16[512,128]{1,0:T(8,128)(2,1)S(1)}, u32[]{:S(2)}, u32[]{:S(2)}) collective-permute-start(bf16[512,128]{1,0:T(8,128)(2,1)S(1)} %get-tuple-element.108), channel_id=1, source_target_pairs={{0,4},{4,0},{8,12},{12,8},{16,20},{20,16},{24,28},{28,24},{1,5},{5... | collective-permute-start | bytes 393224 | tf_op jit(solution)/shard_map/ppermute | solution.py:338
  24.3 2.3 %collective-permute-start.5 = (bf16[128,128]{1,0:T(8,128)(2,1)S(1)}, bf16[128,128]{1,0:T(8,128)(2,1)S(1)}, u32[]{:S(2)}, u32[]{:S(2)}) collective-permute-start(bf16[128,128]{1,0:T(8,128)(2,1)S(1)} %get-tuple-element.81), channel_id=1, source_target_pairs={{0,4},{4,0},{8,12},{12,8},{16,20},{20,16},{24,28},{28,24},{1,5},{5... | collective-permute-start | bytes 98312 | tf_op jit(solution)/shard_map/ppermute | solution.py:384
  24.4 5.6 %collective-permute-start.10 = (bf16[128,128]{1,0:T(8,128)(2,1)S(1)}, bf16[128,128]{1,0:T(8,128)(2,1)S(1)}, u32[]{:S(2)}, u32[]{:S(2)}) collective-permute-start(bf16[128,128]{1,0:T(8,128)(2,1)S(1)} %get-tuple-element.86), channel_id=1, source_target_pairs={{1,2},{3,0},{2,1},{0,3},{5,6},{7,4},{6,5},{4,7},{9,10},{11,8},{10,... | collective-permute-start | bytes 98312 | tf_op jit(solution)/shard_map/ppermute | solution.py:375
  26.6 3.4 %collective-permute-start.9 = (bf16[128,128]{1,0:T(8,128)(2,1)S(1)}, bf16[128,128]{1,0:T(8,128)(2,1)S(1)}, u32[]{:S(2)}, u32[]{:S(2)}) collective-permute-start(bf16[128,128]{1,0:T(8,128)(2,1)S(1)} %get-tuple-element.85), channel_id=1, source_target_pairs={{0,1},{1,0},{2,3},{3,2},{4,5},{5,4},{6,7},{7,6},{8,9},{9,8},{10,11... | collective-permute-start | bytes 98312 | tf_op jit(solution)/shard_map/ppermute | solution.py:374
  26.6 4.0 %collective-permute-start.6 = (bf16[128,128]{1,0:T(8,128)(2,1)S(1)}, bf16[128,128]{1,0:T(8,128)(2,1)S(1)}, u32[]{:S(2)}, u32[]{:S(2)}) collective-permute-start(bf16[128,128]{1,0:T(8,128)(2,1)S(1)} %get-tuple-element.116), channel_id=1, source_target_pairs={{0,12},{4,8},{8,4},{12,0},{16,28},{20,24},{24,20},{28,16},{1,13},{... | collective-permute-start | bytes 98312 | tf_op jit(solution)/shard_map/ppermute | solution.py:338
  26.7 3.9 %collective-permute-start.7 = (bf16[128,128]{1,0:T(8,128)(2,1)S(1)}, bf16[128,128]{1,0:T(8,128)(2,1)S(1)}, u32[]{:S(2)}, u32[]{:S(2)}) collective-permute-start(bf16[128,128]{1,0:T(8,128)(2,1)S(1)} %get-tuple-element.115), channel_id=1, source_target_pairs={{0,16},{4,20},{8,24},{12,28},{16,0},{20,4},{24,8},{28,12},{1,17},{... | collective-permute-start | bytes 98312 | tf_op jit(solution)/shard_map/ppermute | solution.py:338
  27.8 4.2 %collective-permute-start.8 = (bf16[128,128]{1,0:T(8,128)(2,1)S(1)}, bf16[128,128]{1,0:T(8,128)(2,1)S(1)}, u32[]{:S(2)}, u32[]{:S(2)}) collective-permute-start(bf16[128,128]{1,0:T(8,128)(2,1)S(1)} %get-tuple-element.114), channel_id=1, source_target_pairs={{0,28},{4,24},{8,20},{12,16},{16,12},{20,8},{24,4},{28,0},{1,29},{... | collective-permute-start | bytes 98312 | tf_op jit(solution)/shard_map/ppermute | solution.py:338
  29.9 6.2 %collective-permute-start.14 = (bf16[128,128]{1,0:T(8,128)(2,1)S(1)}, bf16[128,128]{1,0:T(8,128)(2,1)S(1)}, u32[]{:S(2)}, u32[]{:S(2)}) collective-permute-start(bf16[128,128]{1,0:T(8,128)(2,1)S(1)} %get-tuple-element.91), channel_id=1, source_target_pairs={{4,8},{12,16},{20,24},{28,0},{8,4},{16,12},{24,20},{0,28},{5,9},{1... | collective-permute-start | bytes 98312 | tf_op jit(solution)/shard_map/ppermute | solution.py:397
  32.1 4.0 %collective-permute-start.11 = (bf16[128,128]{1,0:T(8,128)(2,1)S(1)}, bf16[128,128]{1,0:T(8,128)(2,1)S(1)}, u32[]{:S(2)}, u32[]{:S(2)}) collective-permute-start(bf16[128,128]{1,0:T(8,128)(2,1)S(1)} %add_convert_fusion.2), channel_id=1, source_target_pairs={{0,1},{1,0},{2,3},{3,2},{4,5},{5,4},{6,7},{7,6},{8,9},{9,8},{10,11... | collective-permute-start | bytes 98312 | tf_op jit(solution)/shard_map/ppermute | solution.py:328
  33.9 4.2 %collective-permute-start.12 = (bf16[128,128]{1,0:T(8,128)(2,1)S(1)}, bf16[128,128]{1,0:T(8,128)(2,1)S(1)}, u32[]{:S(2)}, u32[]{:S(2)}) collective-permute-start(bf16[128,128]{1,0:T(8,128)(2,1)S(1)} %add_convert_fusion.2), channel_id=1, source_target_pairs={{0,2},{1,3},{2,0},{3,1},{4,6},{5,7},{6,4},{7,5},{8,10},{9,11},{10,... | collective-permute-start | bytes 98312 | tf_op jit(solution)/shard_map/ppermute | solution.py:328
  33.9 4.6 %collective-permute-start.13 = (bf16[128,128]{1,0:T(8,128)(2,1)S(1)}, bf16[128,128]{1,0:T(8,128)(2,1)S(1)}, u32[]{:S(2)}, u32[]{:S(2)}) collective-permute-start(bf16[128,128]{1,0:T(8,128)(2,1)S(1)} %add_convert_fusion.2), channel_id=1, source_target_pairs={{0,3},{1,2},{2,1},{3,0},{4,7},{5,6},{6,5},{7,4},{8,11},{9,10},{10,... | collective-permute-start | bytes 98312 | tf_op jit(solution)/shard_map/ppermute | solution.py:328
  38.5 5.0 %collective-permute-start.15 = (bf16[128,128]{1,0:T(8,128)(2,1)S(1)}, bf16[128,128]{1,0:T(8,128)(2,1)S(1)}, u32[]{:S(2)}, u32[]{:S(2)}) collective-permute-start(bf16[128,128]{1,0:T(8,128)(2,1)S(1)} %add_convert_fusion.1), channel_id=1, source_target_pairs={{0,12},{4,8},{8,4},{12,0},{16,28},{20,24},{24,20},{28,16},{1,13},{... | collective-permute-start | bytes 98312 | tf_op jit(solution)/shard_map/ppermute | solution.py:343
  41.3 2.8 %collective-permute-start.16 = (bf16[128,128]{1,0:T(8,128)(2,1)S(1)}, bf16[128,128]{1,0:T(8,128)(2,1)S(1)}, u32[]{:S(2)}, u32[]{:S(2)}) collective-permute-start(bf16[128,128]{1,0:T(8,128)(2,1)S(1)} %add_convert_fusion.1), channel_id=1, source_target_pairs={{0,16},{4,20},{8,24},{12,28},{16,0},{20,4},{24,8},{28,12},{1,17},{... | collective-permute-start | bytes 98312 | tf_op jit(solution)/shard_map/ppermute | solution.py:343
  42.3 4.2 %collective-permute-start.17 = (bf16[128,128]{1,0:T(8,128)(2,1)S(1)}, bf16[128,128]{1,0:T(8,128)(2,1)S(1)}, u32[]{:S(2)}, u32[]{:S(2)}) collective-permute-start(bf16[128,128]{1,0:T(8,128)(2,1)S(1)} %add_convert_fusion.1), channel_id=1, source_target_pairs={{0,28},{4,24},{8,20},{12,16},{16,12},{20,8},{24,4},{28,0},{1,29},{... | collective-permute-start | bytes 98312 | tf_op jit(solution)/shard_map/ppermute | solution.py:343
  46.6 0.7 %copy-start = (s32[1,4,128]{2,1,0:T(4,128)S(1)}, s32[1,4,128]{2,1,0:T(4,128)}, u32[]{:S(2)}) copy-start(s32[1,4,128]{2,1,0:T(4,128)} %param.23) | copy-start | bytes 6148
  46.6 1.6 %collective-permute-start.18 = (bf16[512,128]{1,0:T(8,128)(2,1)S(1)}, bf16[512,128]{1,0:T(8,128)(2,1)S(1)}, u32[]{:S(2)}, u32[]{:S(2)}) collective-permute-start(bf16[512,128]{1,0:T(8,128)(2,1)S(1)} %pad_maximum_fusion.1.mine), channel_id=1, source_target_pairs={{0,4},{4,0},{8,12},{12,8},{16,20},{20,16},{24,28},{28,24},{1,5},{5... | collective-permute-start | bytes 393224 | tf_op jit(solution)/shard_map/ppermute | solution.py:493
